TPU v7x, 256 devices: a whole 4x4x8 slice. The times are simulated.
256 devices in a mesh: head: 4 (over z_lo, core), ctx: 64 (over z_hi, x, y).
Axes of the slice: x: 4, y: 4, z: 8 (z_hi: 4, z_lo: 2; z = z_hi * 2 + z_lo), core: 2. Of those that a mesh axis runs over, the one named last changes fastest.
Arguments:
- query: bfloat16 [16384, 16384], P(('head', 'ctx')), may hold values from -5 to 5
- key: bfloat16 [16384, 1024], P(('head', 'ctx')), may hold values from -5 to 5
- value: bfloat16 [16384, 1024], P(('head', 'ctx')), may hold values from -6 to 6
- block_order: int32 [256], replicated, may hold values from 0 to 255, each once
Outputs:
- attended: bfloat16 [16384, 16384], P(('head', 'ctx'))
- log_norm_rows: float32 [16384, 128], P(('head', 'ctx'))
All inputs are finite; a program needn't handle non-finite values.
Results may differ from a plain program's by a relative error of at most 0.0036.
Values may be sent and summed in bfloat16 or wider, within the bound.
A program may use at most 64 MiB of HBM per device.

v0:
```python
import math

import jax
import jax.numpy as jnp
from jax import lax
from jax.sharding import PartitionSpec as P

HEAD_DIMENSION = 128


def passed_along(block, axis, distance):
    devices = range(lax.axis_size(axis))
    route = [((i - distance) % len(devices), i) for i in devices]
    return lax.ppermute(block, axis, route)


def partial_terms(queries, keys, values, query_positions, key_pos):
    rows = queries.shape[0]
    kv_heads = keys.shape[1] // HEAD_DIMENSION
    width = queries.shape[1] // kv_heads
    group = width // HEAD_DIMENSION
    scale = 1.0 / math.sqrt(HEAD_DIMENSION)
    visible = key_pos[None, :] <= query_positions[:, None]
    peaks = []
    totals = []
    accs = []
    for head in range(kv_heads):
        q_head = queries[:, head * width : (head + 1) * width].reshape(rows, group, HEAD_DIMENSION)
        key_head_index = keys[:, head * HEAD_DIMENSION : (head + 1) * HEAD_DIMENSION]
        v_head = values[:, head * HEAD_DIMENSION : (head + 1) * HEAD_DIMENSION]
        score_matrix = (
            jnp.einsum("rgd,kd->grk", q_head, key_head_index, preferred_element_type=jnp.float32)
            * scale
        )
        shifted = jnp.where(visible[None], score_matrix, -1e30)
        peak = jnp.maximum(jnp.max(shifted, axis=-1), -10000.0)
        weights = jnp.exp(shifted - peak[..., None])
        total = jnp.sum(weights, axis=-1)
        probs = weights.astype(jnp.bfloat16)
        acc = jnp.einsum("grk,kd->rgd", probs, v_head, preferred_element_type=jnp.float32)
        peaks.append(peak.T)
        totals.append(total.T)
        accs.append(acc.reshape(rows, width))
    return (
        jnp.concatenate(peaks, axis=1),
        jnp.concatenate(totals, axis=1),
        jnp.concatenate(accs, axis=1),
    )


def combine(first, second):
    peak_a, total_a, acc_a = first
    peak_b, total_b, acc_b = second
    peak = jnp.maximum(peak_a, peak_b)
    factor_a = jnp.exp(peak_a - peak)
    factor_b = jnp.exp(peak_b - peak)
    total = total_a * factor_a + total_b * factor_b
    rows, heads = peak.shape
    acc = (
        acc_a.reshape(rows, heads, -1) * factor_a[..., None]
        + acc_b.reshape(rows, heads, -1) * factor_b[..., None]
    )
    result = (acc / total[..., None]).reshape(rows, -1)
    return (result, peak + jnp.log(total))


def body(query, key, value, block_order):
    n_head = lax.axis_size("head")
    n_ctx = lax.axis_size("ctx")
    block = query.shape[0]
    here_head = lax.axis_index("head")
    here_ctx = lax.axis_index("ctx")
    offsets = jnp.arange(block, dtype=jnp.int32)

    def shard_positions(shard):
        stored = jnp.arange(n_head, dtype=jnp.int32) * n_ctx + shard
        starts = block_order[stored] * block
        return (starts[:, None] + offsets[None, :]).reshape(-1)

    before = (here_ctx - 1) % n_ctx
    local_positions = shard_positions(here_ctx)
    prev_pos = shard_positions(before)
    keys_all, values_all = (
        lax.all_gather(key, "head", axis=0, tiled=True),
        lax.all_gather(value, "head", axis=0, tiled=True),
    )
    keys_prev, values_prev = passed_along((keys_all, values_all), "ctx", 1)
    query_positions = block_order[here_head * n_ctx + here_ctx] * block + offsets
    own = partial_terms(query, keys_all, values_all, query_positions, local_positions)
    far = partial_terms(query, keys_prev, values_prev, query_positions, prev_pos)
    result, lse = combine(own, far)
    return (result.astype(jnp.bfloat16), lse)


def solution(mesh):
    placed = (P(("head", "ctx"), None), P(("head", "ctx"), None), P(("head", "ctx"), None), P())
    return jax.shard_map(
        body,
        mesh=mesh,
        in_specs=placed,
        out_specs=(P(("head", "ctx"), None), P(("head", "ctx"), None)),
        check_vma=False,
    )
```

profile of v0, /device:TPU:55, one launch (start us, length us, event | category | flops | bytes accessed | tf_op | source)
XLA Modules:
  0.0 101.7 jit_solution(6707982960998576785)
XLA Ops:
  0.6 7.9 %all_gather.7 = bf16[256,1024]{1,0:T(8,128)(2,1)} all-gather(bf16[64,1024]{1,0:T(8,128)(2,1)} %param.6), channel_id=1, replica_groups=mesh['head'=4,'ctx'=64] {'head'}, dimensions={0}, use_global_device_ids=true | all-gather | bytes 655360 | tf_op jit(solution)/shard_map/all_gather | solution.py:85
  8.6 1.0 collective-permute-start.1
  9.6 8.0 %all_gather.6 = bf16[256,1024]{1,0:T(8,128)(2,1)S(1)} all-gather(bf16[64,1024]{1,0:T(8,128)(2,1)} %param.5), channel_id=1, replica_groups=mesh['head'=4,'ctx'=64] {'head'}, dimensions={0}, use_global_device_ids=true | all-gather | bytes 655360 | tf_op jit(solution)/shard_map/all_gather | solution.py:84
  17.6 24.2 %collective-permute-start = (bf16[256,1024]{1,0:T(8,128)(2,1)S(1)}, bf16[256,1024]{1,0:T(8,128)(2,1)}, u32[]{:S(2)}, u32[]{:S(2)}) collective-permute-start(bf16[256,1024]{1,0:T(8,128)(2,1)S(1)} %all_gather.6), channel_id=1, source_target_pairs={{63,0},{0,1},{1,2},{2,3},{3,4},{4,5},{5,6},{6,7},{7,8},{8,9},{9,10... | collective-permute-start | bytes 1572872 | tf_op jit(solution)/shard_map/ppermute | solution.py:14
  41.8 1.3 %dynamic_slice.3 = s32[1]{0:T(128)} dynamic-slice(s32[256]{0:T(256)} %param.7, s32[]{:T(128)S(6)} %select_n.80), dynamic_slice_sizes={1} | dynamic-slice | bytes 12 | tf_op jit(solution)/shard_map/dynamic_slice | solution.py:88
  43.8 1.3 %gather_fusion.1 = s32[4]{0:T(128)S(1)} fusion(s32[256]{0:T(256)} %param.7, s32[1024]{0:T(1024)S(1)} %get-tuple-element.50), kind=kCustom, calls=%fused_computation.1 | custom fusion | bytes 48 | tf_op jit(solution)/shard_map/gather | solution.py:77
  45.1 1.3 %gather_fusion = s32[4]{0:T(128)S(1)} fusion(s32[256]{0:T(256)} %param.7, s32[1024]{0:T(1024)S(1)} %get-tuple-element.51), kind=kCustom, calls=%fused_computation | custom fusion | bytes 48 | tf_op jit(solution)/shard_map/gather | solution.py:77
  46.8 1.7 %slice_bitcast_fusion = (bf16[8,16,8,128]{3,2,1,0:T(8,128)(2,1)S(1)}, bf16[8,16,8,128]{3,2,1,0:T(8,128)(2,1)S(1)}, bf16[8,16,8,128]{3,2,1,0:T(8,128)(2,1)S(1)}, ...) fusion(bf16[64,16384]{1,0:T(8,128)(2,1)} %param.4), kind=kLoop, calls=%fused_computation.165 | loop fusion | bytes 4194304
  49.4 1.2 %fusion.48 = f32[64,128,128]{2,0,1:T(8,128)S(1)} fusion(f32[16,64,256]{2,1,0:T(8,128)S(1)} %get-tuple-element.19, f32[16,64]{1,0:T(8,128)S(1)} %broadcast_maximum_fusion.15, bf16[256,1024]{1,0:T(8,128)(2,1)} %all_gather.7), kind=kOutput, calls=%fused_computation.84 | convolution fusion | flops 67633152 | bytes 1642496 | tf_op jit(solution)/shard_map/grk,kd->rgd/dot_general | solution.py:40
  50.6 1.2 %fusion.154 = (f32[16,64]{1,0:T(8,128)S(1)}, f32[16,64,256]{2,1,0:T(8,128)S(1)}) fusion(bf16[8,16,8,128]{3,2,1,0:T(8,128)(2,1)S(1)} %get-tuple-element.8, bf16[256,1024]{1,0:T(8,128)(2,1)} %copy-done.10, pred[64,256]{1,0:T(8,128)(4,1)S(1)} %get-tuple-element.17), kind=kOutput, calls=%fused_computation.294 | convolution fusion | flops 67894272 | bytes 1396736 | tf_op jit(solution)/shard_map/rgd,kd->grk/dot_general | solution.py:32
  51.9 1.2 %fusion.152 = (f32[16,64]{1,0:T(8,128)S(1)}, f32[16,64,256]{2,1,0:T(8,128)S(1)}) fusion(bf16[8,16,8,128]{3,2,1,0:T(8,128)(2,1)S(1)} %get-tuple-element.9, bf16[256,1024]{1,0:T(8,128)(2,1)} %copy-done.10, pred[64,256]{1,0:T(8,128)(4,1)S(1)} %get-tuple-element.17), kind=kOutput, calls=%fused_computation.292 | convolution fusion | flops 67894272 | bytes 1396736 | tf_op jit(solution)/shard_map/rgd,kd->grk/dot_general | solution.py:32
  53.1 1.2 %fusion.151 = (f32[16,64]{1,0:T(8,128)S(1)}, f32[16,64,256]{2,1,0:T(8,128)S(1)}) fusion(bf16[8,16,8,128]{3,2,1,0:T(8,128)(2,1)S(1)} %get-tuple-element.10, bf16[256,1024]{1,0:T(8,128)(2,1)} %copy-done.10, pred[64,256]{1,0:T(8,128)(4,1)S(1)} %get-tuple-element.17), kind=kOutput, calls=%fused_computation.291 | convolution fusion | flops 67894272 | bytes 1396736 | tf_op jit(solution)/shard_map/rgd,kd->grk/dot_general | solution.py:32
  54.4 1.2 %fusion.150 = (f32[16,64]{1,0:T(8,128)S(1)}, f32[16,64,256]{2,1,0:T(8,128)S(1)}) fusion(bf16[8,16,8,128]{3,2,1,0:T(8,128)(2,1)S(1)} %get-tuple-element.11, bf16[256,1024]{1,0:T(8,128)(2,1)} %copy-done.10, pred[64,256]{1,0:T(8,128)(4,1)S(1)} %get-tuple-element.17), kind=kOutput, calls=%fused_computation.290 | convolution fusion | flops 67894272 | bytes 1396736 | tf_op jit(solution)/shard_map/rgd,kd->grk/dot_general | solution.py:32
  55.6 1.2 %fusion.149 = (f32[16,64]{1,0:T(8,128)S(1)}, f32[16,64,256]{2,1,0:T(8,128)S(1)}) fusion(bf16[8,16,8,128]{3,2,1,0:T(8,128)(2,1)S(1)} %get-tuple-element.12, bf16[256,1024]{1,0:T(8,128)(2,1)} %copy-done.10, pred[64,256]{1,0:T(8,128)(4,1)S(1)} %get-tuple-element.17), kind=kOutput, calls=%fused_computation.289 | convolution fusion | flops 67894272 | bytes 1396736 | tf_op jit(solution)/shard_map/rgd,kd->grk/dot_general | solution.py:32
  56.9 1.2 %fusion.148 = (f32[16,64]{1,0:T(8,128)S(1)}, f32[16,64,256]{2,1,0:T(8,128)S(1)}) fusion(bf16[8,16,8,128]{3,2,1,0:T(8,128)(2,1)S(1)} %get-tuple-element.13, bf16[256,1024]{1,0:T(8,128)(2,1)} %copy-done.10, pred[64,256]{1,0:T(8,128)(4,1)S(1)} %get-tuple-element.17), kind=kOutput, calls=%fused_computation.288 | convolution fusion | flops 67894272 | bytes 1396736 | tf_op jit(solution)/shard_map/rgd,kd->grk/dot_general | solution.py:32
  58.1 1.2 %fusion.153 = (f32[16,64]{1,0:T(8,128)S(1)}, f32[16,64,256]{2,1,0:T(8,128)S(1)}) fusion(bf16[8,16,8,128]{3,2,1,0:T(8,128)(2,1)S(1)} %get-tuple-element.15, bf16[256,1024]{1,0:T(8,128)(2,1)} %copy-done.10, pred[64,256]{1,0:T(8,128)(4,1)S(1)} %get-tuple-element.17), kind=kOutput, calls=%fused_computation.293 | convolution fusion | flops 67894272 | bytes 1396736 | tf_op jit(solution)/shard_map/rgd,kd->grk/dot_general | solution.py:32
  59.8 1.2 %fusion.47 = f32[64,128,128]{2,0,1:T(8,128)S(1)} fusion(f32[64,128,128]{2,0,1:T(8,128)S(1)} %fusion.48, f32[16,64,256]{2,1,0:T(8,128)S(1)} %get-tuple-element.21, f32[16,64]{1,0:T(8,128)S(1)} %broadcast_maximum_fusion.14, bf16[256,1024]{1,0:T(8,128)(2,1)} %all_gather.7), kind=kOutput, calls=%fused_computation.82 | convolution fusion | flops 67633152 | bytes 1646592 | tf_op jit(solution)/shard_map/grk,kd->rgd/dot_general | solution.py:40
  61.0 0.4 fusion.53
  61.4 1.2 %fusion.46 = f32[64,128,128]{2,0,1:T(8,128)S(1)} fusion(f32[64,128,128]{2,0,1:T(8,128)S(1)} %fusion.47, f32[16,64,256]{2,1,0:T(8,128)S(1)} %get-tuple-element.23, f32[16,64]{1,0:T(8,128)S(1)} %broadcast_maximum_fusion.13, bf16[256,1024]{1,0:T(8,128)(2,1)} %all_gather.7), kind=kOutput, calls=%fused_computation.80 | convolution fusion | flops 67633152 | bytes 1646592 | tf_op jit(solution)/shard_map/grk,kd->rgd/dot_general | solution.py:40
  63.1 1.2 %fusion.45 = f32[64,128,128]{2,0,1:T(8,128)S(1)} fusion(f32[64,128,128]{2,0,1:T(8,128)S(1)} %fusion.46, f32[16,64,256]{2,1,0:T(8,128)S(1)} %get-tuple-element.25, f32[16,64]{1,0:T(8,128)S(1)} %broadcast_maximum_fusion.12, bf16[256,1024]{1,0:T(8,128)(2,1)} %all_gather.7), kind=kOutput, calls=%fused_computation.78 | convolution fusion | flops 67633152 | bytes 1646592 | tf_op jit(solution)/shard_map/grk,kd->rgd/dot_general | solution.py:40
  64.3 0.4 fusion.57
  64.7 1.2 %fusion.44 = f32[64,128,128]{2,0,1:T(8,128)S(1)} fusion(f32[64,128,128]{2,0,1:T(8,128)S(1)} %fusion.45, f32[16,64,256]{2,1,0:T(8,128)S(1)} %get-tuple-element.27, f32[16,64]{1,0:T(8,128)S(1)} %broadcast_maximum_fusion.11, bf16[256,1024]{1,0:T(8,128)(2,1)} %all_gather.7), kind=kOutput, calls=%fused_computation.76 | convolution fusion | flops 67633152 | bytes 1646592 | tf_op jit(solution)/shard_map/grk,kd->rgd/dot_general | solution.py:40
  66.3 1.2 %fusion.43 = f32[64,128,128]{2,0,1:T(8,128)S(1)} fusion(f32[64,128,128]{2,0,1:T(8,128)S(1)} %fusion.44, f32[16,64,256]{2,1,0:T(8,128)S(1)} %get-tuple-element.29, f32[16,64]{1,0:T(8,128)S(1)} %broadcast_maximum_fusion.10, bf16[256,1024]{1,0:T(8,128)(2,1)} %all_gather.7), kind=kOutput, calls=%fused_computation.74 | convolution fusion | flops 67633152 | bytes 1646592 | tf_op jit(solution)/shard_map/grk,kd->rgd/dot_general | solution.py:40
  67.9 0.4 fusion.61
  68.4 1.2 %fusion.42 = f32[64,128,128]{2,0,1:T(8,128)S(1)} fusion(f32[64,128,128]{2,0,1:T(8,128)S(1)} %fusion.43, f32[16,64,256]{2,1,0:T(8,128)S(1)} %get-tuple-element.31, f32[16,64]{1,0:T(8,128)S(1)} %broadcast_maximum_fusion.9, bf16[256,1024]{1,0:T(8,128)(2,1)} %all_gather.7), kind=kOutput, calls=%fused_computation.72 | convolution fusion | flops 67633152 | bytes 1646592 | tf_op jit(solution)/shard_map/grk,kd->rgd/dot_general | solution.py:40
  69.6 1.2 %fusion.41 = f32[64,128,128]{2,0,1:T(8,128)S(1)} fusion(f32[64,128,128]{2,0,1:T(8,128)S(1)} %fusion.42, f32[16,64,256]{2,1,0:T(8,128)S(1)} %get-tuple-element.33, f32[16,64]{1,0:T(8,128)S(1)} %broadcast_maximum_fusion.8, bf16[256,1024]{1,0:T(8,128)(2,1)} %all_gather.7), kind=kOutput, calls=%fused_computation.70 | convolution fusion | flops 67633152 | bytes 1646592 | tf_op jit(solution)/shard_map/grk,kd->rgd/dot_general | solution.py:40
  70.8 1.3 %fusion.155 = (f32[16,64]{1,0:T(8,128)S(1)}, f32[16,64,256]{2,1,0:T(8,128)S(1)}) fusion(bf16[8,16,8,128]{3,2,1,0:T(8,128)(2,1)S(1)} %get-tuple-element.14, bf16[256,1024]{1,0:T(8,128)(2,1)} %collective-permute-done, pred[64,256]{1,0:T(8,128)(4,1)S(1)} %get-tuple-element.16), kind=kOutput, calls=%fused_computation.295 | convolution fusion | flops 67894272 | bytes 1396736 | tf_op jit(solution)/shard_map/rgd,kd->grk/dot_general | solution.py:32
  72.1 1.3 %fusion.162 = (f32[16,64]{1,0:T(8,128)S(1)}, f32[16,64,256]{2,1,0:T(8,128)S(1)}) fusion(bf16[8,16,8,128]{3,2,1,0:T(8,128)(2,1)S(1)} %get-tuple-element.8, bf16[256,1024]{1,0:T(8,128)(2,1)} %collective-permute-done, pred[64,256]{1,0:T(8,128)(4,1)S(1)} %get-tuple-element.16), kind=kOutput, calls=%fused_computation.302 | convolution fusion | flops 67894272 | bytes 1396736 | tf_op jit(solution)/shard_map/rgd,kd->grk/dot_general | solution.py:32
  73.5 1.2 %fusion.160 = (f32[16,64]{1,0:T(8,128)S(1)}, f32[16,64,256]{2,1,0:T(8,128)S(1)}) fusion(bf16[8,16,8,128]{3,2,1,0:T(8,128)(2,1)S(1)} %get-tuple-element.9, bf16[256,1024]{1,0:T(8,128)(2,1)} %collective-permute-done, pred[64,256]{1,0:T(8,128)(4,1)S(1)} %get-tuple-element.16), kind=kOutput, calls=%fused_computation.300 | convolution fusion | flops 67894272 | bytes 1396736 | tf_op jit(solution)/shard_map/rgd,kd->grk/dot_general | solution.py:32
  74.7 1.2 %fusion.159 = (f32[16,64]{1,0:T(8,128)S(1)}, f32[16,64,256]{2,1,0:T(8,128)S(1)}) fusion(bf16[8,16,8,128]{3,2,1,0:T(8,128)(2,1)S(1)} %get-tuple-element.10, bf16[256,1024]{1,0:T(8,128)(2,1)} %collective-permute-done, pred[64,256]{1,0:T(8,128)(4,1)S(1)} %get-tuple-element.16), kind=kOutput, calls=%fused_computation.299 | convolution fusion | flops 67894272 | bytes 1396736 | tf_op jit(solution)/shard_map/rgd,kd->grk/dot_general | solution.py:32
  76.0 1.3 %fusion.158 = (f32[16,64]{1,0:T(8,128)S(1)}, f32[16,64,256]{2,1,0:T(8,128)S(1)}) fusion(bf16[8,16,8,128]{3,2,1,0:T(8,128)(2,1)S(1)} %get-tuple-element.11, bf16[256,1024]{1,0:T(8,128)(2,1)} %collective-permute-done, pred[64,256]{1,0:T(8,128)(4,1)S(1)} %get-tuple-element.16), kind=kOutput, calls=%fused_computation.298 | convolution fusion | flops 67894272 | bytes 1396736 | tf_op jit(solution)/shard_map/rgd,kd->grk/dot_general | solution.py:32
  77.3 1.3 %fusion.157 = (f32[16,64]{1,0:T(8,128)S(1)}, f32[16,64,256]{2,1,0:T(8,128)S(1)}) fusion(bf16[8,16,8,128]{3,2,1,0:T(8,128)(2,1)S(1)} %get-tuple-element.12, bf16[256,1024]{1,0:T(8,128)(2,1)} %collective-permute-done, pred[64,256]{1,0:T(8,128)(4,1)S(1)} %get-tuple-element.16), kind=kOutput, calls=%fused_computation.297 | convolution fusion | flops 67894272 | bytes 1396736 | tf_op jit(solution)/shard_map/rgd,kd->grk/dot_general | solution.py:32
  78.7 1.3 %fusion.156 = (f32[16,64]{1,0:T(8,128)S(1)}, f32[16,64,256]{2,1,0:T(8,128)S(1)}) fusion(bf16[8,16,8,128]{3,2,1,0:T(8,128)(2,1)S(1)} %get-tuple-element.13, bf16[256,1024]{1,0:T(8,128)(2,1)} %collective-permute-done, pred[64,256]{1,0:T(8,128)(4,1)S(1)} %get-tuple-element.16), kind=kOutput, calls=%fused_computation.296 | convolution fusion | flops 67894272 | bytes 1396736 | tf_op jit(solution)/shard_map/rgd,kd->grk/dot_general | solution.py:32
  80.5 1.2 %fusion.161 = (f32[16,64]{1,0:T(8,128)S(1)}, f32[16,64,256]{2,1,0:T(8,128)S(1)}) fusion(bf16[8,16,8,128]{3,2,1,0:T(8,128)(2,1)S(1)} %get-tuple-element.15, bf16[256,1024]{1,0:T(8,128)(2,1)} %collective-permute-done, pred[64,256]{1,0:T(8,128)(4,1)S(1)} %get-tuple-element.16), kind=kOutput, calls=%fused_computation.301 | convolution fusion | flops 67894272 | bytes 1396736 | tf_op jit(solution)/shard_map/rgd,kd->grk/dot_general | solution.py:32
  81.8 0.4 fusion.75
  83.0 0.4 fusion.69
  83.4 0.6 fusion.67
  84.0 0.4 fusion.77
  84.9 0.7 copy.78
  85.6 1.3 %fusion.40 = f32[64,128,128]{2,0,1:T(8,128)S(1)} fusion(f32[16,64,256]{2,1,0:T(8,128)S(1)} %get-tuple-element.35, f32[16,64]{1,0:T(8,128)S(1)} %broadcast_maximum_fusion.7, bf16[256,1024]{1,0:T(8,128)(2,1)} %collective-permute-done.1), kind=kOutput, calls=%fused_computation.68 | convolution fusion | flops 67633152 | bytes 1642496 | tf_op jit(solution)/shard_map/grk,kd->rgd/dot_general | solution.py:40
  87.0 1.7 %fusion.39 = f32[64,128,128]{2,0,1:T(8,128)S(1)} fusion(f32[64,128,128]{2,0,1:T(8,128)S(1)} %fusion.40, f32[16,64,256]{2,1,0:T(8,128)} %copy-done.5, f32[16,64]{1,0:T(8,128)S(1)} %broadcast_maximum_fusion.6, bf16[256,1024]{1,0:T(8,128)(2,1)} %collective-permute-done.1), kind=kOutput, calls=%fused_computation.66 | convolution fusion | flops 67633152 | bytes 1646592 | tf_op jit(solution)/shard_map/grk,kd->rgd/dot_general | solution.py:40
  88.7 1.6 %fusion.38 = f32[64,128,128]{2,0,1:T(8,128)S(1)} fusion(f32[64,128,128]{2,0,1:T(8,128)S(1)} %fusion.39, f32[16,64,256]{2,1,0:T(8,128)} %copy-done.4, f32[16,64]{1,0:T(8,128)S(1)} %broadcast_maximum_fusion.5, bf16[256,1024]{1,0:T(8,128)(2,1)} %collective-permute-done.1), kind=kOutput, calls=%fused_computation.64 | convolution fusion | flops 67633152 | bytes 1646592 | tf_op jit(solution)/shard_map/grk,kd->rgd/dot_general | solution.py:40
  90.3 1.3 %fusion.37 = f32[64,128,128]{2,0,1:T(8,128)S(1)} fusion(f32[64,128,128]{2,0,1:T(8,128)S(1)} %fusion.38, f32[16,64,256]{2,1,0:T(8,128)S(1)} %copy-done.3, f32[16,64]{1,0:T(8,128)S(1)} %broadcast_maximum_fusion.4, bf16[256,1024]{1,0:T(8,128)(2,1)} %collective-permute-done.1), kind=kOutput, calls=%fused_computation.62 | convolution fusion | flops 67633152 | bytes 1646592 | tf_op jit(solution)/shard_map/grk,kd->rgd/dot_general | solution.py:40
  91.6 1.2 %fusion.36 = f32[64,128,128]{2,0,1:T(8,128)S(1)} fusion(f32[64,128,128]{2,0,1:T(8,128)S(1)} %fusion.37, f32[16,64,256]{2,1,0:T(8,128)S(1)} %copy-done.1, f32[16,64]{1,0:T(8,128)S(1)} %broadcast_maximum_fusion.3, bf16[256,1024]{1,0:T(8,128)(2,1)} %collective-permute-done.1), kind=kOutput, calls=%fused_computation.60 | convolution fusion | flops 67633152 | bytes 1646592 | tf_op jit(solution)/shard_map/grk,kd->rgd/dot_general | solution.py:40
  92.9 1.2 %fusion.35 = f32[64,128,128]{2,0,1:T(8,128)S(1)} fusion(f32[64,128,128]{2,0,1:T(8,128)S(1)} %fusion.36, f32[16,64,256]{2,1,0:T(8,128)S(1)} %get-tuple-element.45, f32[16,64]{1,0:T(8,128)S(1)} %broadcast_maximum_fusion.2, bf16[256,1024]{1,0:T(8,128)(2,1)} %collective-permute-done.1), kind=kOutput, calls=%fused_computation.58 | convolution fusion | flops 67633152 | bytes 1646592 | tf_op jit(solution)/shard_map/grk,kd->rgd/dot_general | solution.py:40
  94.1 1.2 %fusion.34 = f32[64,128,128]{2,0,1:T(8,128)S(1)} fusion(f32[64,128,128]{2,0,1:T(8,128)S(1)} %fusion.35, f32[16,64,256]{2,1,0:T(8,128)S(1)} %copy-done.7, f32[16,64]{1,0:T(8,128)S(1)} %broadcast_maximum_fusion.1, bf16[256,1024]{1,0:T(8,128)(2,1)} %collective-permute-done.1), kind=kOutput, calls=%fused_computation.56 | convolution fusion | flops 67633152 | bytes 1646592 | tf_op jit(solution)/shard_map/grk,kd->rgd/dot_general | solution.py:40
  95.3 1.2 %fusion.33 = f32[64,128,128]{2,0,1:T(8,128)S(1)} fusion(f32[64,128,128]{2,0,1:T(8,128)S(1)} %fusion.34, f32[16,64,256]{2,1,0:T(8,128)S(1)} %get-tuple-element.49, f32[16,64]{1,0:T(8,128)S(1)} %broadcast_maximum_fusion, bf16[256,1024]{1,0:T(8,128)(2,1)} %collective-permute-done.1), kind=kOutput, calls=%fused_computation.54 | convolution fusion | flops 67633152 | bytes 1646592 | tf_op jit(solution)/shard_map/grk,kd->rgd/dot_general | solution.py:40
  96.5 5.2 %copy_bitcast_fusion = bf16[64,16384]{1,0:T(8,128)(2,1)} fusion(f32[64,128]{0,1:T(8,128)S(1)} %get-tuple-element.5, f32[64,128,128]{2,0,1:T(8,128)S(1)} %fusion.33, f32[64,128]{0,1:T(8,128)S(1)} %get-tuple-element.7, f32[64,128,128]{2,0,1:T(8,128)S(1)} %copy-done.9, f32[64,128]{0,1:T(8,128)S(1)} %get-tuple-element.6), kind=kLoop, calls=%fused_computation.3 | loop fusion | flops 5242880 | bytes 10584064 | tf_op jit(solution)/shard_map/convert_element_type | solution.py:92
  (94 shorter events, 4.7 us)
Async XLA Ops:
  8.6 77.1 %collective-permute-start.1 = (bf16[256,1024]{1,0:T(8,128)(2,1)}, bf16[256,1024]{1,0:T(8,128)(2,1)}, u32[]{:S(2)}, u32[]{:S(2)}) collective-permute-start(bf16[256,1024]{1,0:T(8,128)(2,1)} %all_gather.7), channel_id=1, source_target_pairs={{63,0},{0,1},{1,2},{2,3},{3,4},{4,5},{5,6},{6,7},{7,8},{8,9},{9,10... | collective-permute-start | bytes 1572872 | tf_op jit(solution)/shard_map/ppermute | solution.py:14
  17.6 33.0 %copy-start.10 = (bf16[256,1024]{1,0:T(8,128)(2,1)}, bf16[256,1024]{1,0:T(8,128)(2,1)S(1)}, u32[]{:S(2)}) copy-start(bf16[256,1024]{1,0:T(8,128)(2,1)S(1)} %all_gather.6) | copy-start | bytes 1572868
  17.6 53.2 %collective-permute-start = (bf16[256,1024]{1,0:T(8,128)(2,1)S(1)}, bf16[256,1024]{1,0:T(8,128)(2,1)}, u32[]{:S(2)}, u32[]{:S(2)}) collective-permute-start(bf16[256,1024]{1,0:T(8,128)(2,1)S(1)} %all_gather.6), channel_id=1, source_target_pairs={{63,0},{0,1},{1,2},{2,3},{3,4},{4,5},{5,6},{6,7},{7,8},{8,9},{9,10... | collective-permute-start | bytes 1572872 | tf_op jit(solution)/shard_map/ppermute | solution.py:14
  70.8 7.9 %copy-start.8 = (f32[64,128,128]{2,0,1:T(8,128)}, f32[64,128,128]{2,0,1:T(8,128)S(1)}, u32[]{:S(2)}) copy-start(f32[64,128,128]{2,0,1:T(8,128)S(1)} %fusion.41) | copy-start | bytes 12582916
  75.9 6.6 %copy-start = (f32[16,64,256]{2,1,0:T(8,128)}, f32[16,64,256]{2,1,0:T(8,128)S(1)}, u32[]{:S(2)}) copy-start(f32[16,64,256]{2,1,0:T(8,128)S(1)} %get-tuple-element.43) | copy-start | bytes 3145732
  77.3 5.7 %copy-start.2 = (f32[16,64,256]{2,1,0:T(8,128)}, f32[16,64,256]{2,1,0:T(8,128)S(1)}, u32[]{:S(2)}) copy-start(f32[16,64,256]{2,1,0:T(8,128)S(1)} %get-tuple-element.41) | copy-start | bytes 3145732
  78.6 5.3 %copy-start.4 = (f32[16,64,256]{2,1,0:T(8,128)}, f32[16,64,256]{2,1,0:T(8,128)S(1)}, u32[]{:S(2)}) copy-start(f32[16,64,256]{2,1,0:T(8,128)S(1)} %get-tuple-element.39) | copy-start | bytes 3145732
  80.0 4.5 %copy-start.5 = (f32[16,64,256]{2,1,0:T(8,128)}, f32[16,64,256]{2,1,0:T(8,128)S(1)}, u32[]{:S(2)}) copy-start(f32[16,64,256]{2,1,0:T(8,128)S(1)} %get-tuple-element.37) | copy-start | bytes 3145732
  81.7 2.7 %copy-start.6 = (f32[16,64,256]{2,1,0:T(8,128)}, f32[16,64,256]{2,1,0:T(8,128)S(1)}, u32[]{:S(2)}) copy-start(f32[16,64,256]{2,1,0:T(8,128)S(1)} %get-tuple-element.47) | copy-start | bytes 3145732
  85.6 4.6 %copy-start.3 = (f32[16,64,256]{2,1,0:T(8,128)S(1)}, f32[16,64,256]{2,1,0:T(8,128)}, u32[]{:S(2)}) copy-start(f32[16,64,256]{2,1,0:T(8,128)} %copy-done.2) | copy-start | bytes 3145732
  85.6 6.0 %copy-start.1 = (f32[16,64,256]{2,1,0:T(8,128)S(1)}, f32[16,64,256]{2,1,0:T(8,128)}, u32[]{:S(2)}) copy-start(f32[16,64,256]{2,1,0:T(8,128)} %copy-done) | copy-start | bytes 3145732
  87.0 7.1 %copy-start.7 = (f32[16,64,256]{2,1,0:T(8,128)S(1)}, f32[16,64,256]{2,1,0:T(8,128)}, u32[]{:S(2)}) copy-start(f32[16,64,256]{2,1,0:T(8,128)} %copy-done.6) | copy-start | bytes 3145732
  90.3 6.2 %copy-start.9 = (f32[64,128,128]{2,0,1:T(8,128)S(1)}, f32[64,128,128]{2,0,1:T(8,128)}, u32[]{:S(2)}) copy-start(f32[64,128,128]{2,0,1:T(8,128)} %copy-done.8) | copy-start | bytes 12582916
where the time goes:
time: 103 us; the launch traced here: 102 us
  matrix products  39.5 us (38%)
  starting transfers between devices  25.2 us (24%)
  blocking collectives  15.9 us (15%)
  other arithmetic  12.2 us (12%)
  local copies, waits for them, and re-layouts  6.61 us (6%)
  between operations  2.19 us (2%)
    ppermute x2, starting transfers between devices, passed_along(): return lax.ppermute(block, axis, route)  25.2 us
    dot_general x16, matrix products, partial_terms(): jnp.einsum('grk,kd->rgd', probs, v_head, preferred_element_type=jnp.float32)  20.3 us
    dot_general x16, matrix products, partial_terms(): jnp.einsum('rgd,kd->grk', q_head, key_head_index, preferred_element_type=...  19.2 us
    all_gather x1, blocking collectives, body(): lax.all_gather(key, 'head', axis=0, tiled=True)  8 us
    all_gather x1, blocking collectives, body(): lax.all_gather(value, 'head', axis=0, tiled=True)  7.94 us
    reduce_sum x16, other arithmetic, partial_terms(): total = jnp.sum(weights, axis=-1)  6.53 us
    convert_element_type x1, other arithmetic, body(): return (result.astype(jnp.bfloat16), lse)  5.21 us
    gather x2, local copies, waits for them, and re-layouts, shard_positions(): starts = block_order[stored] * block  2.64 us
  transfers between devices with their start and end apart: 2, of which 0 were waited for; matrix products, arithmetic and copies ran while one was open for 42% of the time, Pallas kernels for 0%

commit v1 on v0

v1 whole, which is shorter than its diff:
```python
import functools
import math

import jax
import jax.numpy as jnp
from jax import lax
from jax.experimental import pallas as pl
from jax.experimental.pallas import tpu as pltpu
from jax.sharding import PartitionSpec as P

D = 128
KV = 8
PLANE = 16
SLOTS = 8
HIDDEN = -1e30
MESH = pl.DeviceIdType.MESH


def kernel(n_ctx, order_hbm, q_hbm, k_hbm, v_hbm, out_ref, lse_ref,
           order, q_s, kv, s_s, p_s, o_s, mask_s, l_s, m_s,
           order_sem, q_sem, own_sem, send_sem, recv_sem):
    rows = q_hbm.shape[0]
    width = q_hbm.shape[1] // KV
    group = width // D
    hd = lax.axis_index("head")
    ctx = lax.axis_index("ctx")
    z, c = hd // 2, hd % 2
    nxt, prv = (ctx + 1) % n_ctx, (ctx + n_ctx - 1) % n_ctx
    partner = (2 * z + 1 - c, ctx)
    across = (2 * (1 - z) + c, ctx)
    first = ctx % PLANE == 0
    last = ctx % PLANE == PLANE - 1
    silent = jnp.logical_and(last, z == 0)
    ahead = jnp.logical_not(silent)
    second = jnp.logical_and(last, z == 1)
    own_target = (hd, nxt)
    z_target = (jnp.where(second, c, hd), nxt)
    z_slot = jnp.where(second, 4, 6)
    source = jnp.where(first, 2 + c, hd)

    def chunk(slot, j):
        return kv.at[j, :, pl.ds(slot * rows, rows)]

    def message(kind, j, src, dst, device):
        return pltpu.make_async_remote_copy(
            src_ref=chunk(src, j), dst_ref=chunk(dst, j),
            send_sem=send_sem.at[kind, j], recv_sem=recv_sem.at[dst, j],
            device_id=device, device_id_type=MESH)

    def own_partner(j):
        return message(1, j, 0, 1, partner)

    def own_across(j):
        return message(2, j, 0, 2, across)

    def across_partner(j):
        return message(3, j, 2, 3, partner)

    def own_ahead(j):
        return message(4, j, 0, 4, own_target)

    def far_partner(j):
        return message(5, j, 4, 5, partner)

    def across_ahead(j):
        return message(6, j, 2, z_slot, z_target)

    def far_across(j):
        return message(0, j, 4, 6, across)

    def last_partner(j):
        return message(7, j, 6, 7, partner)

    def arrived(slot, j):
        message(1, j, 0, slot, partner).wait_recv()

    def q_copy(j):
        return pltpu.make_async_copy(
            q_hbm.at[:, pl.ds(pl.multiple_of(j * width, width), width)], q_s.at[j], q_sem.at[j])

    def own_copy(i, j):
        ref = (k_hbm, v_hbm)[i]
        return pltpu.make_async_copy(
            ref.at[:, pl.ds(pl.multiple_of(j * D, D), D)],
            kv.at[j, i, pl.ds(0, rows)], own_sem.at[i, j])

    for j in range(KV):
        own_copy(0, j).start()
        own_copy(1, j).start()
    order_copy = pltpu.make_async_copy(order_hbm, order, order_sem)
    order_copy.start()
    for j in range(KV):
        q_copy(j).start()

    barrier = pltpu.get_barrier_semaphore()

    def greet(device):
        pl.semaphore_signal(barrier, inc=1, device_id=device, device_id_type=MESH)

    greet(partner)
    greet(across)
    greet((source, prv))

    @pl.when(ahead)
    def _():
        greet(own_target)

    @pl.when(second)
    def _():
        greet(z_target)

    peers = 3 + jnp.where(ahead, 1, 0) + jnp.where(second, 1, 0)
    pl.semaphore_wait(barrier, peers)

    for j in range(KV):
        own_copy(0, j).wait()
        own_copy(1, j).wait()
        own_across(j).start()
        if j < 3:
            @pl.when(ahead)
            def _(j=j):
                own_ahead(j).start()
        own_partner(j).start()

    order_copy.wait()
    query_pos = order[hd * n_ctx + ctx] * rows + lax.broadcasted_iota(jnp.int32, (rows, D), 1)
    for slot in range(SLOTS):
        holder = 2 * (z if slot % 4 < 2 else 1 - z) + (c if slot % 2 == 0 else 1 - c)
        block = order[holder * n_ctx + (ctx if slot < 4 else prv)]
        key_pos = block * rows + lax.broadcasted_iota(jnp.int32, (rows, D), 0)
        mask_s[slot * rows:(slot + 1) * rows, :] = jnp.where(
            key_pos <= query_pos, 0.0, HIDDEN).astype(jnp.bfloat16)
    lane = lax.broadcasted_iota(jnp.int32, (rows, D), 1)
    row = lax.broadcasted_iota(jnp.int32, (rows, D), 0)
    pick = jnp.where(lane == row, 1.0, 0.0).astype(jnp.bfloat16)
    picks = jnp.concatenate([pick] * group, axis=0)
    ones = jnp.ones((SLOTS * rows, D), jnp.bfloat16)
    l_s[...] = jnp.ones_like(l_s)
    m_s[...] = jnp.zeros_like(m_s)

    def pass_across(j):
        arrived(2, j)

        @pl.when(ahead)
        def _():
            across_ahead(j).start()

        across_partner(j).start()

    def pass_far(j):
        arrived(4, j)

        @pl.when(first)
        def _():
            far_across(j).start()

        far_partner(j).start()
        arrived(6, j)
        last_partner(j).start()

    pass_across(0)
    pass_across(1)
    pass_far(0)

    scale = 1.0 / math.sqrt(D)
    floor = -10000.0 / scale
    factor = scale * math.log2(math.e)

    def step(j, carry):
        @pl.when(j < KV - 2)
        def _():
            pass_across(j + 2)

        @pl.when(jnp.logical_and(ahead, j < KV - 3))
        def _():
            own_ahead(j + 3).start()

        @pl.when(j < KV - 1)
        def _():
            pass_far(j + 1)

        q_copy(j).wait()
        arrived(1, j)
        arrived(3, j)
        arrived(5, j)
        arrived(7, j)
        heads = [q_s[j, :, i * D:(i + 1) * D] for i in range(group)]
        q = jnp.concatenate([jnp.concatenate(heads, axis=0), picks], axis=1)
        k = jnp.concatenate([kv[j, 0], mask_s[...]], axis=1)
        v = jnp.concatenate([kv[j, 1], ones], axis=1)
        s_s[...] = lax.dot_general(q, k, (((1,), (1,)), ((), ())),
                                   preferred_element_type=jnp.float32)
        total, top = l_s[...], m_s[...]
        peaks = []
        for i in range(group):
            s = s_s[i * rows:(i + 1) * rows, :]
            peak = jnp.maximum(jnp.max(s, axis=1, keepdims=True), floor)
            p_s[i * rows:(i + 1) * rows, :] = jnp.exp2((s - peak) * factor).astype(jnp.bfloat16)
            top = jnp.where(lane == j * group + i, peak, top)
        o_s[...] = jnp.dot(p_s[...], v, preferred_element_type=jnp.float32)
        for i in range(group):
            acc = o_s[i * rows:(i + 1) * rows, :D]
            sums = o_s[i * rows:(i + 1) * rows, D:]
            out_ref[:, pl.ds(pl.multiple_of((j * group + i) * D, D), D)] = (acc / sums).astype(jnp.bfloat16)
            total = jnp.where(lane == j * group + i, sums, total)
        l_s[...] = total
        m_s[...] = top
        return carry

    lax.fori_loop(0, KV, step, 0)
    lse_ref[...] = m_s[...] * scale + jnp.log(l_s[...])

    def drain(j, carry):
        own_across(j).wait_send()
        own_partner(j).wait_send()
        across_partner(j).wait_send()
        far_partner(j).wait_send()
        last_partner(j).wait_send()

        @pl.when(ahead)
        def _():
            own_ahead(j).wait_send()
            across_ahead(j).wait_send()

        @pl.when(first)
        def _():
            far_across(j).wait_send()

        return carry

    lax.fori_loop(0, KV, drain, 0)


def body(query, key, value, block_order):
    n_ctx = lax.axis_size("ctx")
    rows = query.shape[0]
    heads = query.shape[1] // D
    group = heads // KV
    keys = SLOTS * rows
    vmem, smem, hbm = pltpu.VMEM, pltpu.SMEM, pltpu.HBM
    dma = pltpu.SemaphoreType.DMA
    args = [pltpu.with_memory_space_constraint(x, hbm) for x in (block_order, query, key, value)]
    out, lse = pl.pallas_call(
        functools.partial(kernel, n_ctx),
        out_shape=(
            jax.ShapeDtypeStruct(query.shape, jnp.bfloat16),
            jax.ShapeDtypeStruct((rows, heads), jnp.float32),
        ),
        in_specs=[
            pl.BlockSpec(memory_space=hbm),
            pl.BlockSpec(memory_space=hbm),
            pl.BlockSpec(memory_space=hbm),
            pl.BlockSpec(memory_space=hbm),
        ],
        out_specs=(pl.BlockSpec(memory_space=vmem), pl.BlockSpec(memory_space=vmem)),
        scratch_shapes=[
            smem(block_order.shape, jnp.int32),
            vmem((KV, rows, group * D), jnp.bfloat16),
            vmem((KV, 2, keys, D), jnp.bfloat16),
            vmem((group * rows, keys), jnp.float32),
            vmem((group * rows, keys), jnp.bfloat16),
            vmem((group * rows, 2 * D), jnp.float32),
            vmem((keys, D), jnp.bfloat16),
            vmem((rows, heads), jnp.float32),
            vmem((rows, heads), jnp.float32),
            dma,
            dma((KV,)),
            dma((2, KV)),
            dma((8, KV)),
            dma((8, KV)),
        ],
        compiler_params=pltpu.CompilerParams(
            collective_id=0, has_side_effects=True, vmem_limit_bytes=40 * 1024 * 1024
        ),
        cost_estimate=pl.CostEstimate(
            flops=4 * rows * heads * keys * D,
            bytes_accessed=4 * rows * heads * D,
            transcendentals=rows * heads * keys,
        ),
    )(*args)
    return out, lse


def solution(mesh):
    placed = (P(("head", "ctx"), None), P(("head", "ctx"), None), P(("head", "ctx"), None), P())
    return jax.shard_map(
        body,
        mesh=mesh,
        in_specs=placed,
        out_specs=(P(("head", "ctx"), None), P(("head", "ctx"), None)),
        check_vma=False,
    )
```

time: 103 us -> 57.2 us (0.56)
  the two profiles are of different devices: /device:TPU:55 before, /device:TPU:1 now
where the time goes in v1:
time: 57.2 us; the launch traced here: 57.1 us
  Pallas kernels  54.5 us (95%)
  local copies, waits for them, and re-layouts  1.94 us (3%)
  between operations  0.64 us (1%)
    pallas_call x1, Pallas kernels, body(): pl.pallas_call(functools.partial(kernel, n_ctx), out_shape=(jax.ShapeDtyp...  54.5 us
    unnamed x2, local copies, waits for them, and re-layouts  1.94 us

profile of v1, /device:TPU:1, one launch (start us, length us, event | category | flops | bytes accessed | tf_op | source)
XLA Modules:
  0.0 57.1 jit_solution(1618766357731274572)
XLA Ops:
  0.6 54.5 %shard_map.59 = (bf16[64,16384]{1,0:T(8,128)(2,1)S(1)}, f32[64,128]{1,0:T(8,128)S(1)}) custom-call(s32[256]{0:T(256)} %order_hbm.1, bf16[64,16384]{1,0:T(8,128)(2,1)} %q_hbm.1, bf16[64,1024]{1,0:T(8,128)(2,1)} %k_hbm.1, bf16[64,1024]{1,0:T(8,128)(2,1)} %v_hbm.1), custom_call_target="tpu_custom_call" | custom-call | flops 2147483648 | bytes 4194304 | tf_op jit(solution)/shard_map/pallas_call | solution.py:243
  55.1 1.3 %copy.8 = bf16[64,16384]{1,0:T(8,128)(2,1)} copy(bf16[64,16384]{1,0:T(8,128)(2,1)S(1)} %get-tuple-element.4) | data formatting | bytes 4194304
  56.5 0.6 %copy.9 = f32[64,128]{1,0:T(8,128)} copy(f32[64,128]{1,0:T(8,128)S(1)} %get-tuple-element.5) | data formatting | bytes 65536

commit v2 on v1

--- a/solution.py
+++ b/solution.py
@@ -11,13 +11,16 @@
 D = 128
 KV = 8
 PLANE = 16
+AHEAD = 3
+LEAD = 2
+READY = 4
 SLOTS = 8
 HIDDEN = -1e30
 MESH = pl.DeviceIdType.MESH
 
 
 def kernel(n_ctx, order_hbm, q_hbm, k_hbm, v_hbm, out_ref, lse_ref,
-           order, q_s, kv, s_s, p_s, o_s, mask_s, l_s, m_s,
+           order, q_s, kv, s_s, p_s, m_s, o_s, f_s, far_s, mask_s, lse_l, lse_m,
            order_sem, q_sem, own_sem, send_sem, recv_sem):
     rows = q_hbm.shape[0]
     width = q_hbm.shape[1] // KV
@@ -30,13 +33,17 @@
     across = (2 * (1 - z) + c, ctx)
     first = ctx % PLANE == 0
     last = ctx % PLANE == PLANE - 1
-    silent = jnp.logical_and(last, z == 0)
-    ahead = jnp.logical_not(silent)
+    ahead = jnp.logical_not(jnp.logical_and(last, z == 0))
     second = jnp.logical_and(last, z == 1)
+    forwards = jnp.logical_or(first, second)
+    crosses = jnp.logical_not(jnp.logical_or(first, last))
+    from_cross = jnp.logical_not(jnp.logical_or(first, ctx % PLANE == 1))
     own_target = (hd, nxt)
+    cross_target = (2 * (1 - z) + c, nxt)
     z_target = (jnp.where(second, c, hd), nxt)
     z_slot = jnp.where(second, 4, 6)
     source = jnp.where(first, 2 + c, hd)
+    cross_source = (2 * (1 - z) + c, prv)
 
     def chunk(slot, j):
         return kv.at[j, :, pl.ds(slot * rows, rows)]
@@ -64,6 +71,9 @@
 
     def across_ahead(j):
         return message(6, j, 2, z_slot, z_target)
+
+    def own_cross(j):
+        return message(6, j, 0, 6, cross_target)
 
     def far_across(j):
         return message(0, j, 4, 6, across)
@@ -101,25 +111,30 @@
     greet(across)
     greet((source, prv))
 
-    @pl.when(ahead)
+    @pl.when(from_cross)
     def _():
-        greet(own_target)
-
-    @pl.when(second)
-    def _():
-        greet(z_target)
-
-    peers = 3 + jnp.where(ahead, 1, 0) + jnp.where(second, 1, 0)
-    pl.semaphore_wait(barrier, peers)
-
+        greet(cross_source)
+
+    def one(flag):
+        return jnp.where(flag, 1, 0)
+
+    pl.semaphore_wait(barrier, 2 + one(ahead) + one(second) + one(crosses))
+
+    early = jnp.logical_and(ahead, jnp.logical_not(second))
+    early = jnp.logical_and(ahead, jnp.logical_not(second))
     for j in range(KV):
         own_copy(0, j).wait()
         own_copy(1, j).wait()
         own_across(j).start()
-        if j < 3:
-            @pl.when(ahead)
-            def _(j=j):
-                own_ahead(j).start()
+
+        @pl.when(crosses)
+        def _(j=j):
+            own_cross(j).start()
+
+        @pl.when(early if j >= LEAD else ahead)
+        def _(j=j):
+            own_ahead(j).start()
+
         own_partner(j).start()
 
     order_copy.wait()
@@ -133,17 +148,19 @@
     lane = lax.broadcasted_iota(jnp.int32, (rows, D), 1)
     row = lax.broadcasted_iota(jnp.int32, (rows, D), 0)
     pick = jnp.where(lane == row, 1.0, 0.0).astype(jnp.bfloat16)
-    picks = jnp.concatenate([pick] * group, axis=0)
-    ones = jnp.ones((SLOTS * rows, D), jnp.bfloat16)
-    l_s[...] = jnp.ones_like(l_s)
-    m_s[...] = jnp.zeros_like(m_s)
+    lse_l[...] = jnp.ones_like(lse_l)
+    lse_m[...] = jnp.zeros_like(lse_m)
 
     def pass_across(j):
         arrived(2, j)
 
-        @pl.when(ahead)
+        @pl.when(forwards)
         def _():
             across_ahead(j).start()
+
+        @pl.when(jnp.logical_and(second, j < KV - LEAD))
+        def _():
+            own_ahead(j + LEAD).start()
 
         across_partner(j).start()
 
@@ -155,60 +172,112 @@
             far_across(j).start()
 
         far_partner(j).start()
+
+    def pass_last(j):
         arrived(6, j)
         last_partner(j).start()
-
-    pass_across(0)
-    pass_across(1)
-    pass_far(0)
 
     scale = 1.0 / math.sqrt(D)
     floor = -10000.0 / scale
     factor = scale * math.log2(math.e)
-
-    def step(j, carry):
+    keys = SLOTS // 2 * rows
+    parts = [range(group // 2), range(group // 2, group)]
+    picks = jnp.concatenate([pick] * (group // 2), axis=0)
+    ones = jnp.ones((keys, D), jnp.bfloat16)
+
+    def scores(j, shard):
+        seen = pl.ds(shard * keys, keys)
+        k = jnp.concatenate([kv[j, 0, seen], mask_s[seen]], axis=1)
+        for part, heads in enumerate(parts):
+            q = jnp.concatenate([q_s[j, :, i * D:(i + 1) * D] for i in heads], axis=0)
+            s_s[part] = lax.dot_general(
+                jnp.concatenate([q, picks], axis=1), k, (((1,), (1,)), ((), ())),
+                preferred_element_type=jnp.float32)
+
+    def value(j, shard):
+        return jnp.concatenate([kv[j, 1, shard * keys:(shard + 1) * keys], ones], axis=1)
+
+    def own_step(j, carry):
         @pl.when(j < KV - 2)
         def _():
             pass_across(j + 2)
 
-        @pl.when(jnp.logical_and(ahead, j < KV - 3))
-        def _():
-            own_ahead(j + 3).start()
-
-        @pl.when(j < KV - 1)
-        def _():
-            pass_far(j + 1)
+        @pl.when(jnp.logical_and(jnp.logical_not(first), j >= KV - READY))
+        def _():
+            pass_far(j - (KV - READY))
+            pass_last(j - (KV - READY))
 
         q_copy(j).wait()
         arrived(1, j)
         arrived(3, j)
+        scores(j, 0)
+        v = value(j, 0)
+        for part, heads in enumerate(parts):
+            for n, i in enumerate(heads):
+                at = slice(n * rows, (n + 1) * rows)
+                s = s_s[part, at]
+                peak = jnp.maximum(jnp.max(s, axis=1, keepdims=True), floor)
+                p_s[part, at] = jnp.exp2((s - peak) * factor).astype(jnp.bfloat16)
+                m_s[j, i] = jnp.broadcast_to(peak, (rows, D))
+            o_s[j, part] = jnp.dot(p_s[part], v, preferred_element_type=jnp.float32)
+        return carry
+
+    def far_step(j, carry):
+        later = jnp.logical_not(first)
+
+        @pl.when(jnp.logical_and(first, j < KV - AHEAD))
+        def _():
+            pass_far(j + AHEAD)
+
+        @pl.when(jnp.logical_and(later, jnp.logical_and(j >= READY - 1, j < KV - 1)))
+        def _():
+            pass_far(j + 1)
+
+        @pl.when(jnp.logical_and(jnp.logical_or(first, j >= READY - 1), j < KV - 1))
+        def _():
+            pass_last(j + 1)
+
         arrived(5, j)
         arrived(7, j)
-        heads = [q_s[j, :, i * D:(i + 1) * D] for i in range(group)]
-        q = jnp.concatenate([jnp.concatenate(heads, axis=0), picks], axis=1)
-        k = jnp.concatenate([kv[j, 0], mask_s[...]], axis=1)
-        v = jnp.concatenate([kv[j, 1], ones], axis=1)
-        s_s[...] = lax.dot_general(q, k, (((1,), (1,)), ((), ())),
-                                   preferred_element_type=jnp.float32)
-        total, top = l_s[...], m_s[...]
-        peaks = []
-        for i in range(group):
-            s = s_s[i * rows:(i + 1) * rows, :]
-            peak = jnp.maximum(jnp.max(s, axis=1, keepdims=True), floor)
-            p_s[i * rows:(i + 1) * rows, :] = jnp.exp2((s - peak) * factor).astype(jnp.bfloat16)
-            top = jnp.where(lane == j * group + i, peak, top)
-        o_s[...] = jnp.dot(p_s[...], v, preferred_element_type=jnp.float32)
-        for i in range(group):
-            acc = o_s[i * rows:(i + 1) * rows, :D]
-            sums = o_s[i * rows:(i + 1) * rows, D:]
-            out_ref[:, pl.ds(pl.multiple_of((j * group + i) * D, D), D)] = (acc / sums).astype(jnp.bfloat16)
-            total = jnp.where(lane == j * group + i, sums, total)
-        l_s[...] = total
-        m_s[...] = top
+        scores(j, 1)
+        v = value(j, 1)
+        total, top = lse_l[...], lse_m[...]
+        for part, heads in enumerate(parts):
+            for n, i in enumerate(heads):
+                at = slice(n * rows, (n + 1) * rows)
+                s = s_s[part, at]
+                peak = jnp.maximum(m_s[j, i], jnp.max(s, axis=1, keepdims=True))
+                p = [jnp.exp2((s[:, at * D:(at + 1) * D] - peak) * factor).astype(jnp.bfloat16)
+                     for at in range(keys // D)]
+                p_s[part, at] = jnp.concatenate(p, axis=1)
+                f_s[part, at] = jnp.exp2((m_s[j, i] - peak) * factor)
+                top = jnp.where(lane == j * group + i, peak, top)
+            far_s[part] = jnp.dot(p_s[part], v, preferred_element_type=jnp.float32)
+        for part, heads in enumerate(parts):
+            for n, i in enumerate(heads):
+                at = slice(n * rows, (n + 1) * rows)
+                kept = f_s[part, at]
+                acc = o_s[j, part, at, :D] * kept + far_s[part, at, :D]
+                sums = o_s[j, part, at, D:] * kept + far_s[part, at, D:]
+                out_ref[:, pl.ds(pl.multiple_of((j * group + i) * D, D), D)] = (
+                    acc / sums).astype(jnp.bfloat16)
+                total = jnp.where(lane == j * group + i, sums, total)
+        lse_l[...] = total
+        lse_m[...] = top
         return carry
 
-    lax.fori_loop(0, KV, step, 0)
-    lse_ref[...] = m_s[...] * scale + jnp.log(l_s[...])
+    pass_across(0)
+    pass_across(1)
+    lax.fori_loop(0, KV, own_step, 0)
+
+    @pl.when(first)
+    def _():
+        for j in range(AHEAD):
+            pass_far(j)
+        pass_last(0)
+
+    lax.fori_loop(0, KV, far_step, 0)
+    lse_ref[...] = lse_m[...] * scale + jnp.log(lse_l[...])
 
     def drain(j, carry):
         own_across(j).wait_send()
@@ -220,6 +289,13 @@
         @pl.when(ahead)
         def _():
             own_ahead(j).wait_send()
+
+        @pl.when(crosses)
+        def _():
+            own_cross(j).wait_send()
+
+        @pl.when(forwards)
+        def _():
             across_ahead(j).wait_send()
 
         @pl.when(first)
@@ -237,6 +313,7 @@
     heads = query.shape[1] // D
     group = heads // KV
     keys = SLOTS * rows
+    half = group * rows // 2
     vmem, smem, hbm = pltpu.VMEM, pltpu.SMEM, pltpu.HBM
     dma = pltpu.SemaphoreType.DMA
     args = [pltpu.with_memory_space_constraint(x, hbm) for x in (block_order, query, key, value)]
@@ -257,9 +334,12 @@
             smem(block_order.shape, jnp.int32),
             vmem((KV, rows, group * D), jnp.bfloat16),
             vmem((KV, 2, keys, D), jnp.bfloat16),
-            vmem((group * rows, keys), jnp.float32),
-            vmem((group * rows, keys), jnp.bfloat16),
-            vmem((group * rows, 2 * D), jnp.float32),
+            vmem((2, half, keys // 2), jnp.float32),
+            vmem((2, half, keys // 2), jnp.bfloat16),
+            vmem((KV, group, rows, D), jnp.float32),
+            vmem((KV, 2, half, 2 * D), jnp.float32),
+            vmem((2, half, D), jnp.float32),
+            vmem((2, half, 2 * D), jnp.float32),
             vmem((keys, D), jnp.bfloat16),
             vmem((rows, heads), jnp.float32),
             vmem((rows, heads), jnp.float32),

time: 57.2 us -> 37.4 us (0.65)
  Pallas kernels: 54.5 us -> 34.7 us
    pallas_call x1, Pallas kernels: 54.5 us -> 34.7 us  [body(): pl.pallas_call(functools.partial(kernel, n_ctx), out_shape=(jax.ShapeDtyp...]
where the time goes in v2:
time: 37.4 us; the launch traced here: 37.3 us
  Pallas kernels  34.7 us (93%)
  local copies, waits for them, and re-layouts  1.94 us (5%)
  between operations  0.64 us (2%)
    pallas_call x1, Pallas kernels, body(): pl.pallas_call(functools.partial(kernel, n_ctx), out_shape=(jax.ShapeDtyp...  34.7 us
    unnamed x2, local copies, waits for them, and re-layouts  1.94 us

profile of v2, /device:TPU:1, one launch (start us, length us, event | category | flops | bytes accessed | tf_op | source)
XLA Modules:
  0.0 37.3 jit_solution(8886287929675461700)
XLA Ops:
  0.6 34.7 %shard_map.59 = (bf16[64,16384]{1,0:T(8,128)(2,1)S(1)}, f32[64,128]{1,0:T(8,128)S(1)}) custom-call(s32[256]{0:T(256)} %order_hbm.1, bf16[64,16384]{1,0:T(8,128)(2,1)} %q_hbm.1, bf16[64,1024]{1,0:T(8,128)(2,1)} %k_hbm.1, bf16[64,1024]{1,0:T(8,128)(2,1)} %v_hbm.1), custom_call_target="tpu_custom_call" | custom-call | flops 2147483648 | bytes 4194304 | tf_op jit(solution)/shard_map/pallas_call | solution.py:320
  35.4 1.3 %copy.8 = bf16[64,16384]{1,0:T(8,128)(2,1)} copy(bf16[64,16384]{1,0:T(8,128)(2,1)S(1)} %get-tuple-element.4) | data formatting | bytes 4194304
  36.7 0.6 %copy.9 = f32[64,128]{1,0:T(8,128)} copy(f32[64,128]{1,0:T(8,128)S(1)} %get-tuple-element.5) | data formatting | bytes 65536

commit v3 on v2

--- a/solution.py
+++ b/solution.py
@@ -12,15 +12,15 @@
 KV = 8
 PLANE = 16
 AHEAD = 3
-LEAD = 2
+RELAY = 3
 READY = 4
 SLOTS = 8
 HIDDEN = -1e30
 MESH = pl.DeviceIdType.MESH
 
 
-def kernel(n_ctx, order_hbm, q_hbm, k_hbm, v_hbm, out_ref, lse_ref,
-           order, q_s, kv, s_s, p_s, m_s, o_s, f_s, far_s, mask_s, lse_l, lse_m,
+def kernel(n_ctx, order_hbm, q_hbm, k_hbm, v_hbm, out_ref, lse_l, lse_m,
+           order, q_s, kv, relay_s, s_s, p_s, m_s, o_s, f_s, far_s, mask_s,
            order_sem, q_sem, own_sem, send_sem, recv_sem):
     rows = q_hbm.shape[0]
     width = q_hbm.shape[1] // KV
@@ -35,14 +35,21 @@
     last = ctx % PLANE == PLANE - 1
     ahead = jnp.logical_not(jnp.logical_and(last, z == 0))
     second = jnp.logical_and(last, z == 1)
-    forwards = jnp.logical_or(first, second)
-    crosses = jnp.logical_not(jnp.logical_or(first, last))
-    from_cross = jnp.logical_not(jnp.logical_or(first, ctx % PLANE == 1))
+    spare = ctx % PLANE == RELAY
+    relays = jnp.logical_and(spare, z == 1)
+    by_relay = jnp.logical_and(first, z == 1)
+    forwards = jnp.logical_or(jnp.logical_or(first, spare), second)
+    crosses = jnp.logical_not(jnp.logical_or(jnp.logical_or(first, spare), last))
+    from_cross = jnp.logical_not(jnp.logical_or(
+        first, jnp.logical_or(ctx % PLANE == 1, ctx % PLANE == RELAY + 1)))
     own_target = (hd, nxt)
     cross_target = (2 * (1 - z) + c, nxt)
     z_target = (jnp.where(second, c, hd), nxt)
     z_slot = jnp.where(second, 4, 6)
-    source = jnp.where(first, 2 + c, hd)
+    source = (jnp.where(first, 2 + c, hd), jnp.where(by_relay, prv - (PLANE - 1 - RELAY), prv))
+    relay_source = (hd, ctx + PLANE - 1 - RELAY)
+    relay_stop = (hd, ctx - (PLANE - 1 - RELAY))
+    relay_target = (hd, (ctx + PLANE - RELAY) % n_ctx)
     cross_source = (2 * (1 - z) + c, prv)
 
     def chunk(slot, j):
@@ -71,6 +78,18 @@
 
     def across_ahead(j):
         return message(6, j, 2, z_slot, z_target)
+
+    def to_relay(j):
+        return pltpu.make_async_remote_copy(
+            src_ref=chunk(0, j), dst_ref=relay_s.at[j],
+            send_sem=send_sem.at[4, j], recv_sem=recv_sem.at[8, j],
+            device_id=relay_stop, device_id_type=MESH)
+
+    def from_relay(j):
+        return pltpu.make_async_remote_copy(
+            src_ref=relay_s.at[j], dst_ref=chunk(4, j),
+            send_sem=send_sem.at[8, j], recv_sem=recv_sem.at[4, j],
+            device_id=relay_target, device_id_type=MESH)
 
     def own_cross(j):
         return message(6, j, 0, 6, cross_target)
@@ -109,7 +128,11 @@
 
     greet(partner)
     greet(across)
-    greet((source, prv))
+    greet(source)
+
+    @pl.when(relays)
+    def _():
+        greet(relay_source)
 
     @pl.when(from_cross)
     def _():
@@ -118,7 +141,7 @@
     def one(flag):
         return jnp.where(flag, 1, 0)
 
-    pl.semaphore_wait(barrier, 2 + one(ahead) + one(second) + one(crosses))
+    pl.semaphore_wait(barrier, 2 + one(ahead) + one(second) + one(crosses) + one(relays))
 
     early = jnp.logical_and(ahead, jnp.logical_not(second))
     early = jnp.logical_and(ahead, jnp.logical_not(second))
@@ -131,9 +154,13 @@
         def _(j=j):
             own_cross(j).start()
 
-        @pl.when(early if j >= LEAD else ahead)
+        @pl.when(early)
         def _(j=j):
             own_ahead(j).start()
+
+        @pl.when(second)
+        def _(j=j):
+            to_relay(j).start()
 
         own_partner(j).start()
 
@@ -158,10 +185,6 @@
         def _():
             across_ahead(j).start()
 
-        @pl.when(jnp.logical_and(second, j < KV - LEAD))
-        def _():
-            own_ahead(j + LEAD).start()
-
         across_partner(j).start()
 
     def pass_far(j):
@@ -172,6 +195,10 @@
             far_across(j).start()
 
         far_partner(j).start()
+
+    def pass_relay(j):
+        to_relay(j).wait_recv()
+        from_relay(j).start()
 
     def pass_last(j):
         arrived(6, j)
@@ -201,6 +228,10 @@
         @pl.when(j < KV - 2)
         def _():
             pass_across(j + 2)
+
+            @pl.when(relays)
+            def _():
+                pass_relay(j + 2)
 
         @pl.when(jnp.logical_and(jnp.logical_not(first), j >= KV - READY))
         def _():
@@ -266,8 +297,13 @@
         lse_m[...] = top
         return carry
 
-    pass_across(0)
-    pass_across(1)
+    for j in range(2):
+        pass_across(j)
+
+        @pl.when(relays)
+        def _(j=j):
+            pass_relay(j)
+
     lax.fori_loop(0, KV, own_step, 0)
 
     @pl.when(first)
@@ -277,8 +313,6 @@
         pass_last(0)
 
     lax.fori_loop(0, KV, far_step, 0)
-    lse_ref[...] = lse_m[...] * scale + jnp.log(lse_l[...])
-
     def drain(j, carry):
         own_across(j).wait_send()
         own_partner(j).wait_send()
@@ -290,6 +324,10 @@
         def _():
             own_ahead(j).wait_send()
 
+        @pl.when(relays)
+        def _():
+            from_relay(j).wait_send()
+
         @pl.when(crosses)
         def _():
             own_cross(j).wait_send()
@@ -305,6 +343,24 @@
         return carry
 
     lax.fori_loop(0, KV, drain, 0)
+
+
+def finish(out_ref, total, top, out_hbm, lse_hbm, lse_s, out_sem, lse_sem):
+    width = out_ref.shape[1] // KV
+    copies = [
+        pltpu.make_async_copy(
+            out_ref.at[:, j * width:(j + 1) * width],
+            out_hbm.at[:, j * width:(j + 1) * width], out_sem.at[j])
+        for j in range(KV)
+    ]
+    for copy in copies:
+        copy.start()
+    lse_s[...] = top[...] * (1.0 / math.sqrt(D)) + jnp.log(total[...])
+    lse_copy = pltpu.make_async_copy(lse_s, lse_hbm, lse_sem)
+    lse_copy.start()
+    for copy in copies:
+        copy.wait()
+    lse_copy.wait()
 
 
 def body(query, key, value, block_order):
@@ -317,11 +373,13 @@
     vmem, smem, hbm = pltpu.VMEM, pltpu.SMEM, pltpu.HBM
     dma = pltpu.SemaphoreType.DMA
     args = [pltpu.with_memory_space_constraint(x, hbm) for x in (block_order, query, key, value)]
-    out, lse = pl.pallas_call(
+    stats = jax.ShapeDtypeStruct((rows, heads), jnp.float32)
+    out, total, top = pl.pallas_call(
         functools.partial(kernel, n_ctx),
         out_shape=(
             jax.ShapeDtypeStruct(query.shape, jnp.bfloat16),
-            jax.ShapeDtypeStruct((rows, heads), jnp.float32),
+            stats,
+            stats,
         ),
         in_specs=[
             pl.BlockSpec(memory_space=hbm),
@@ -329,11 +387,12 @@
             pl.BlockSpec(memory_space=hbm),
             pl.BlockSpec(memory_space=hbm),
         ],
-        out_specs=(pl.BlockSpec(memory_space=vmem), pl.BlockSpec(memory_space=vmem)),
+        out_specs=(pl.BlockSpec(memory_space=vmem),) * 3,
         scratch_shapes=[
             smem(block_order.shape, jnp.int32),
             vmem((KV, rows, group * D), jnp.bfloat16),
             vmem((KV, 2, keys, D), jnp.bfloat16),
+            vmem((KV, 2, rows, D), jnp.bfloat16),
             vmem((2, half, keys // 2), jnp.float32),
             vmem((2, half, keys // 2), jnp.bfloat16),
             vmem((KV, group, rows, D), jnp.float32),
@@ -341,13 +400,11 @@
             vmem((2, half, D), jnp.float32),
             vmem((2, half, 2 * D), jnp.float32),
             vmem((keys, D), jnp.bfloat16),
-            vmem((rows, heads), jnp.float32),
-            vmem((rows, heads), jnp.float32),
             dma,
             dma((KV,)),
             dma((2, KV)),
-            dma((8, KV)),
-            dma((8, KV)),
+            dma((9, KV)),
+            dma((9, KV)),
         ],
         compiler_params=pltpu.CompilerParams(
             collective_id=0, has_side_effects=True, vmem_limit_bytes=40 * 1024 * 1024
@@ -358,7 +415,14 @@
             transcendentals=rows * heads * keys,
         ),
     )(*args)
-    return out, lse
+    return pl.pallas_call(
+        finish,
+        out_shape=(jax.ShapeDtypeStruct(query.shape, jnp.bfloat16), stats),
+        in_specs=[pl.BlockSpec(memory_space=vmem)] * 3,
+        out_specs=(pl.BlockSpec(memory_space=hbm),) * 2,
+        scratch_shapes=[vmem((rows, heads), jnp.float32), dma((KV,)), dma],
+        compiler_params=pltpu.CompilerParams(vmem_limit_bytes=4 * 1024 * 1024),
+    )(out, total, top)
 
 
 def solution(mesh):

time: 37.4 us -> 34.5 us (0.922)
  local copies, waits for them, and re-layouts: 1.94 us -> 0 us
  Pallas kernels: 34.7 us -> 33.8 us
    pallas_call x1, Pallas kernels: 34.7 us -> 32.4 us  [body(): pl.pallas_call(functools.partial(kernel, n_ctx), out_shape=(jax.ShapeDtyp...]
    unnamed x2 -> x0, local copies, waits for them, and re-layouts: 1.94 us -> none
    pallas_call x0 -> x1, Pallas kernels: none -> 1.39 us  [body(): pl.pallas_call(finish, out_shape=(jax.ShapeDtypeStruct(query.shape, jnp.b...]
where the time goes in v3:
time: 34.5 us; the launch traced here: 34.4 us
  Pallas kernels  33.8 us (98%)
  between operations  0.64 us (2%)
    pallas_call x1, Pallas kernels, body(): pl.pallas_call(functools.partial(kernel, n_ctx), out_shape=(jax.ShapeDtyp...  32.4 us
    pallas_call x1, Pallas kernels, body(): pl.pallas_call(finish, out_shape=(jax.ShapeDtypeStruct(query.shape, jnp.b...  1.39 us

profile of v3, /device:TPU:1, one launch (start us, length us, event | category | flops | bytes accessed | tf_op | source)
XLA Modules:
  0.0 34.4 jit_solution(9689591070524624088)
XLA Ops:
  0.6 32.4 %shard_map.59 = (bf16[64,16384]{1,0:T(8,128)(2,1)S(1)}, f32[64,128]{1,0:T(8,128)S(1)}, f32[64,128]{1,0:T(8,128)S(1)}) custom-call(s32[256]{0:T(256)} %order_hbm.1, bf16[64,16384]{1,0:T(8,128)(2,1)} %q_hbm.1, bf16[64,1024]{1,0:T(8,128)(2,1)} %k_hbm.1, bf16[64,1024]{1,0:T(8,128)(2,1)} %v_hbm.1), custom_call_target="tpu_custom_call" | custom-call | flops 2147483648 | bytes 4194304 | tf_op jit(solution)/shard_map/pallas_call | solution.py:377
  33.0 1.4 %shard_map.60 = (bf16[64,16384]{1,0:T(8,128)(2,1)}, f32[64,128]{1,0:T(8,128)}) custom-call(bf16[64,16384]{1,0:T(8,128)(2,1)S(1)} %get-tuple-element.5.out_ref, f32[64,128]{1,0:T(8,128)S(1)} %get-tuple-element.6.total, f32[64,128]{1,0:T(8,128)S(1)} %get-tuple-element.7.top), custom_call_target="tpu_custom_call" | custom-call | tf_op jit(solution)/shard_map/pallas_call | solution.py:418

commit v4 on v3

--- a/solution.py
+++ b/solution.py
@@ -11,8 +11,9 @@
 D = 128
 KV = 8
 PLANE = 16
-AHEAD = 3
+AHEAD = 5
 RELAY = 3
+DIRECT = 6
 READY = 4
 SLOTS = 8
 HIDDEN = -1e30
@@ -31,26 +32,27 @@
     nxt, prv = (ctx + 1) % n_ctx, (ctx + n_ctx - 1) % n_ctx
     partner = (2 * z + 1 - c, ctx)
     across = (2 * (1 - z) + c, ctx)
+    diagonal = (2 * (1 - z) + 1 - c, ctx)
     first = ctx % PLANE == 0
     last = ctx % PLANE == PLANE - 1
-    ahead = jnp.logical_not(jnp.logical_and(last, z == 0))
-    second = jnp.logical_and(last, z == 1)
-    spare = ctx % PLANE == RELAY
+    shard = ctx % PLANE
+    spare = shard == RELAY
     relays = jnp.logical_and(spare, z == 1)
+    split = jnp.logical_and(last, z == 1)
+    ahead = jnp.logical_not(split)
+    crowded = jnp.logical_and(last, z == 0)
     by_relay = jnp.logical_and(first, z == 1)
-    forwards = jnp.logical_or(jnp.logical_or(first, spare), second)
-    crosses = jnp.logical_not(jnp.logical_or(jnp.logical_or(first, spare), last))
+    forwards = jnp.logical_or(first, spare)
+    crosses = jnp.logical_not(jnp.logical_or(forwards, last))
+    before = prv % PLANE
     from_cross = jnp.logical_not(jnp.logical_or(
-        first, jnp.logical_or(ctx % PLANE == 1, ctx % PLANE == RELAY + 1)))
+        jnp.logical_or(before == 0, before == PLANE - 1), before == RELAY))
     own_target = (hd, nxt)
     cross_target = (2 * (1 - z) + c, nxt)
-    z_target = (jnp.where(second, c, hd), nxt)
-    z_slot = jnp.where(second, 4, 6)
-    source = (jnp.where(first, 2 + c, hd), jnp.where(by_relay, prv - (PLANE - 1 - RELAY), prv))
-    relay_source = (hd, ctx + PLANE - 1 - RELAY)
-    relay_stop = (hd, ctx - (PLANE - 1 - RELAY))
-    relay_target = (hd, (ctx + PLANE - RELAY) % n_ctx)
     cross_source = (2 * (1 - z) + c, prv)
+    source = (hd, jnp.where(by_relay, prv - (PLANE - 1 - RELAY), prv))
+    relay_source = (hd, ctx - shard + PLANE - 1)
+    relay_target = (hd, (ctx - shard + PLANE) % n_ctx)
 
     def chunk(slot, j):
         return kv.at[j, :, pl.ds(slot * rows, rows)]
@@ -77,13 +79,14 @@
         return message(5, j, 4, 5, partner)
 
     def across_ahead(j):
-        return message(6, j, 2, z_slot, z_target)
+        return message(6, j, 2, 6, own_target)
 
     def to_relay(j):
+        stop = ctx - (PLANE - 1 - RELAY)
         return pltpu.make_async_remote_copy(
             src_ref=chunk(0, j), dst_ref=relay_s.at[j],
             send_sem=send_sem.at[4, j], recv_sem=recv_sem.at[8, j],
-            device_id=relay_stop, device_id_type=MESH)
+            device_id=(hd, stop), device_id_type=MESH)
 
     def from_relay(j):
         return pltpu.make_async_remote_copy(
@@ -99,6 +102,12 @@
 
     def last_partner(j):
         return message(7, j, 6, 7, partner)
+
+    def far_diagonal(j):
+        return message(7, j, 4, 7, diagonal)
+
+    def direct(j):
+        return jnp.logical_and(first, j >= DIRECT)
 
     def arrived(slot, j):
         message(1, j, 0, slot, partner).wait_recv()
@@ -134,6 +143,10 @@
     def _():
         greet(relay_source)
 
+    @pl.when(first)
+    def _():
+        greet(diagonal)
+
     @pl.when(from_cross)
     def _():
         greet(cross_source)
@@ -141,28 +154,35 @@
     def one(flag):
         return jnp.where(flag, 1, 0)
 
-    pl.semaphore_wait(barrier, 2 + one(ahead) + one(second) + one(crosses) + one(relays))
-
-    early = jnp.logical_and(ahead, jnp.logical_not(second))
-    early = jnp.logical_and(ahead, jnp.logical_not(second))
+    pl.semaphore_wait(
+        barrier, 2 + one(ahead) + one(split) + one(crosses) + one(relays) + one(first))
+
     for j in range(KV):
         own_copy(0, j).wait()
         own_copy(1, j).wait()
-        own_across(j).start()
+
+        @pl.when(jnp.logical_not(crowded))
+        def _(j=j):
+            own_across(j).start()
 
         @pl.when(crosses)
         def _(j=j):
             own_cross(j).start()
 
-        @pl.when(early)
+        @pl.when(ahead)
         def _(j=j):
             own_ahead(j).start()
 
-        @pl.when(second)
+        @pl.when(split)
         def _(j=j):
             to_relay(j).start()
 
         own_partner(j).start()
+
+    @pl.when(crowded)
+    def _():
+        for j in range(KV):
+            own_across(j).start()
 
     order_copy.wait()
     query_pos = order[hd * n_ctx + ctx] * rows + lax.broadcasted_iota(jnp.int32, (rows, D), 1)
@@ -194,6 +214,10 @@
         def _():
             far_across(j).start()
 
+        @pl.when(direct(j))
+        def _():
+            far_diagonal(j).start()
+
         far_partner(j).start()
 
     def pass_relay(j):
@@ -201,8 +225,10 @@
         from_relay(j).start()
 
     def pass_last(j):
-        arrived(6, j)
-        last_partner(j).start()
+        @pl.when(jnp.logical_not(direct(j)))
+        def _():
+            arrived(6, j)
+            last_partner(j).start()
 
     scale = 1.0 / math.sqrt(D)
     floor = -10000.0 / scale
@@ -267,6 +293,10 @@
         @pl.when(jnp.logical_and(jnp.logical_or(first, j >= READY - 1), j < KV - 1))
         def _():
             pass_last(j + 1)
+
+        @pl.when(direct(j))
+        def _():
+            arrived(6, j)
 
         arrived(5, j)
         arrived(7, j)
@@ -323,6 +353,10 @@
         @pl.when(ahead)
         def _():
             own_ahead(j).wait_send()
+
+        @pl.when(split)
+        def _():
+            to_relay(j).wait_send()
 
         @pl.when(relays)
         def _():

time: 34.5 us -> 32.2 us (0.933)
  Pallas kernels: 33.8 us -> 31.4 us
    pallas_call x1, Pallas kernels: 32.4 us -> 30 us  [body(): pl.pallas_call(functools.partial(kernel, n_ctx), out_shape=(jax.ShapeDtyp...]
where the time goes in v4:
time: 32.2 us; the launch traced here: 32.1 us
  Pallas kernels  31.4 us (98%)
  between operations  0.64 us (2%)
    pallas_call x1, Pallas kernels, body(): pl.pallas_call(functools.partial(kernel, n_ctx), out_shape=(jax.ShapeDtyp...  30 us
    pallas_call x1, Pallas kernels, body(): pl.pallas_call(finish, out_shape=(jax.ShapeDtypeStruct(query.shape, jnp.b...  1.39 us

profile of v4, /device:TPU:1, one launch (start us, length us, event | category | flops | bytes accessed | tf_op | source)
XLA Modules:
  0.0 32.1 jit_solution(16366667954578600705)
XLA Ops:
  0.6 30.0 %shard_map.59 = (bf16[64,16384]{1,0:T(8,128)(2,1)S(1)}, f32[64,128]{1,0:T(8,128)S(1)}, f32[64,128]{1,0:T(8,128)S(1)}) custom-call(s32[256]{0:T(256)} %order_hbm.1, bf16[64,16384]{1,0:T(8,128)(2,1)} %q_hbm.1, bf16[64,1024]{1,0:T(8,128)(2,1)} %k_hbm.1, bf16[64,1024]{1,0:T(8,128)(2,1)} %v_hbm.1), custom_call_target="tpu_custom_call" | custom-call | flops 2147483648 | bytes 4194304 | tf_op jit(solution)/shard_map/pallas_call | solution.py:411
  30.7 1.4 %shard_map.60 = (bf16[64,16384]{1,0:T(8,128)(2,1)}, f32[64,128]{1,0:T(8,128)}) custom-call(bf16[64,16384]{1,0:T(8,128)(2,1)S(1)} %get-tuple-element.5.out_ref, f32[64,128]{1,0:T(8,128)S(1)} %get-tuple-element.6.total, f32[64,128]{1,0:T(8,128)S(1)} %get-tuple-element.7.top), custom_call_target="tpu_custom_call" | custom-call | tf_op jit(solution)/shard_map/pallas_call | solution.py:452

commit v5 on v4

--- a/solution.py
+++ b/solution.py
@@ -13,14 +13,52 @@
 PLANE = 16
 AHEAD = 5
 RELAY = 3
-DIRECT = 6
+DIRECT = 4
 READY = 4
 SLOTS = 8
 HIDDEN = -1e30
 MESH = pl.DeviceIdType.MESH
 
 
+def score(s_s, heads, part, q, picks, k):
+    q = jnp.concatenate([q[:, i * D:(i + 1) * D] for i in heads], axis=0)
+    s_s[part] = lax.dot_general(
+        jnp.concatenate([q, picks], axis=1), k, (((1,), (1,)), ((), ())),
+        preferred_element_type=jnp.float32)
+
+
+def attend_far(base, group, rows, v, m, o, s_s, p_s, f_s, far_s, total, top, out_ref, column=None):
+    factor = math.log2(math.e) / math.sqrt(D)
+    column = base if column is None else column
+    parts = [range(group // 2), range(group // 2, group)]
+    lane = lax.broadcasted_iota(jnp.int32, (rows, D), 1)
+    for part, heads in enumerate(parts):
+        for n, i in enumerate(heads):
+            at = slice(n * rows, (n + 1) * rows)
+            s = s_s[part, at]
+            peak = jnp.maximum(m[i], jnp.max(s, axis=1, keepdims=True))
+            p = [jnp.exp2((s[:, at * D:(at + 1) * D] - peak) * factor).astype(jnp.bfloat16)
+                 for at in range(s.shape[1] // D)]
+            p_s[part, at] = jnp.concatenate(p, axis=1)
+            f_s[part, at] = jnp.exp2((m[i] - peak) * factor)
+            top = jnp.where(lane == base + i, peak, top)
+        far_s[part] = jnp.dot(p_s[part], v, preferred_element_type=jnp.float32)
+    for part, heads in enumerate(parts):
+        for n, i in enumerate(heads):
+            at = slice(n * rows, (n + 1) * rows)
+            kept = f_s[part, at]
+            acc = o[part, at, :D] * kept + far_s[part, at, :D]
+            sums = o[part, at, D:] * kept + far_s[part, at, D:]
+            start = (column + i) * D
+            if not isinstance(start, int):
+                start = pl.multiple_of(start, D)
+            out_ref[:, pl.ds(start, D)] = (acc / sums).astype(jnp.bfloat16)
+            total = jnp.where(lane == base + i, sums, total)
+    return total, top
+
+
 def kernel(n_ctx, order_hbm, q_hbm, k_hbm, v_hbm, out_ref, lse_l, lse_m,
+           q_last, o_last, m_last, kv_last, mask_last,
            order, q_s, kv, relay_s, s_s, p_s, m_s, o_s, f_s, far_s, mask_s,
            order_sem, q_sem, own_sem, send_sem, recv_sem):
     rows = q_hbm.shape[0]
@@ -242,10 +280,7 @@
         seen = pl.ds(shard * keys, keys)
         k = jnp.concatenate([kv[j, 0, seen], mask_s[seen]], axis=1)
         for part, heads in enumerate(parts):
-            q = jnp.concatenate([q_s[j, :, i * D:(i + 1) * D] for i in heads], axis=0)
-            s_s[part] = lax.dot_general(
-                jnp.concatenate([q, picks], axis=1), k, (((1,), (1,)), ((), ())),
-                preferred_element_type=jnp.float32)
+            score(s_s, heads, part, q_s.at[j], picks, k)
 
     def value(j, shard):
         return jnp.concatenate([kv[j, 1, shard * keys:(shard + 1) * keys], ones], axis=1)
@@ -301,28 +336,9 @@
         arrived(5, j)
         arrived(7, j)
         scores(j, 1)
-        v = value(j, 1)
-        total, top = lse_l[...], lse_m[...]
-        for part, heads in enumerate(parts):
-            for n, i in enumerate(heads):
-                at = slice(n * rows, (n + 1) * rows)
-                s = s_s[part, at]
-                peak = jnp.maximum(m_s[j, i], jnp.max(s, axis=1, keepdims=True))
-                p = [jnp.exp2((s[:, at * D:(at + 1) * D] - peak) * factor).astype(jnp.bfloat16)
-                     for at in range(keys // D)]
-                p_s[part, at] = jnp.concatenate(p, axis=1)
-                f_s[part, at] = jnp.exp2((m_s[j, i] - peak) * factor)
-                top = jnp.where(lane == j * group + i, peak, top)
-            far_s[part] = jnp.dot(p_s[part], v, preferred_element_type=jnp.float32)
-        for part, heads in enumerate(parts):
-            for n, i in enumerate(heads):
-                at = slice(n * rows, (n + 1) * rows)
-                kept = f_s[part, at]
-                acc = o_s[j, part, at, :D] * kept + far_s[part, at, :D]
-                sums = o_s[j, part, at, D:] * kept + far_s[part, at, D:]
-                out_ref[:, pl.ds(pl.multiple_of((j * group + i) * D, D), D)] = (
-                    acc / sums).astype(jnp.bfloat16)
-                total = jnp.where(lane == j * group + i, sums, total)
+        total, top = attend_far(
+            j * group, group, rows, value(j, 1), m_s.at[j], o_s.at[j], s_s, p_s, f_s, far_s,
+            lse_l[...], lse_m[...], out_ref)
         lse_l[...] = total
         lse_m[...] = top
         return carry
@@ -335,6 +351,11 @@
             pass_relay(j)
 
     lax.fori_loop(0, KV, own_step, 0)
+
+    q_last[...] = q_s[KV - 1]
+    o_last[...] = o_s[KV - 1]
+    m_last[...] = m_s[KV - 1]
+    mask_last[...] = mask_s[keys:]
 
     @pl.when(first)
     def _():
@@ -342,7 +363,17 @@
             pass_far(j)
         pass_last(0)
 
-    lax.fori_loop(0, KV, far_step, 0)
+    lax.fori_loop(0, KV - 1, far_step, 0)
+
+    end = KV - 1
+
+    @pl.when(direct(end))
+    def _():
+        arrived(6, end)
+
+    arrived(5, end)
+    arrived(7, end)
+    kv_last[...] = kv[end, :, keys:]
     def drain(j, carry):
         own_across(j).wait_send()
         own_partner(j).wait_send()
@@ -379,21 +410,39 @@
     lax.fori_loop(0, KV, drain, 0)
 
 
-def finish(out_ref, total, top, out_hbm, lse_hbm, lse_s, out_sem, lse_sem):
-    width = out_ref.shape[1] // KV
+def finish(out_ref, total, top, q, o, m, kv, mask, out_hbm, lse_hbm,
+           tail_s, lse_s, s_s, p_s, f_s, far_s, out_sem, tail_sem, lse_sem):
+    rows, width = q.shape
+    group = width // D
+    done = out_ref.shape[1] // width
     copies = [
         pltpu.make_async_copy(
             out_ref.at[:, j * width:(j + 1) * width],
             out_hbm.at[:, j * width:(j + 1) * width], out_sem.at[j])
-        for j in range(KV)
+        for j in range(done)
     ]
     for copy in copies:
         copy.start()
-    lse_s[...] = top[...] * (1.0 / math.sqrt(D)) + jnp.log(total[...])
+    lane = lax.broadcasted_iota(jnp.int32, (rows, D), 1)
+    row = lax.broadcasted_iota(jnp.int32, (rows, D), 0)
+    picks = jnp.concatenate(
+        [jnp.where(lane == row, 1.0, 0.0).astype(jnp.bfloat16)] * (group // 2), axis=0)
+    k = jnp.concatenate([kv[0], mask[...]], axis=1)
+    v = jnp.concatenate([kv[1], jnp.ones(mask.shape, jnp.bfloat16)], axis=1)
+    for part in range(2):
+        score(s_s, range(part * group // 2, (part + 1) * group // 2), part, q, picks, k)
+    sums, peaks = attend_far(
+        done * group, group, rows, v, m, o, s_s, p_s, f_s, far_s,
+        total[...], top[...], tail_s, column=0)
+    tail = pltpu.make_async_copy(
+        tail_s, out_hbm.at[:, done * width:(done + 1) * width], tail_sem)
+    tail.start()
+    lse_s[...] = peaks * (1.0 / math.sqrt(D)) + jnp.log(sums)
     lse_copy = pltpu.make_async_copy(lse_s, lse_hbm, lse_sem)
     lse_copy.start()
     for copy in copies:
         copy.wait()
+    tail.wait()
     lse_copy.wait()
 
 
@@ -408,12 +457,23 @@
     dma = pltpu.SemaphoreType.DMA
     args = [pltpu.with_memory_space_constraint(x, hbm) for x in (block_order, query, key, value)]
     stats = jax.ShapeDtypeStruct((rows, heads), jnp.float32)
-    out, total, top = pl.pallas_call(
+    work = [
+        vmem((2, half, keys // 2), jnp.float32),
+        vmem((2, half, keys // 2), jnp.bfloat16),
+        vmem((2, half, D), jnp.float32),
+        vmem((2, half, 2 * D), jnp.float32),
+    ]
+    handed = pl.pallas_call(
         functools.partial(kernel, n_ctx),
         out_shape=(
-            jax.ShapeDtypeStruct(query.shape, jnp.bfloat16),
+            jax.ShapeDtypeStruct((rows, (KV - 1) * group * D), jnp.bfloat16),
             stats,
             stats,
+            jax.ShapeDtypeStruct((rows, group * D), jnp.bfloat16),
+            jax.ShapeDtypeStruct((2, half, 2 * D), jnp.float32),
+            jax.ShapeDtypeStruct((group, rows, D), jnp.float32),
+            jax.ShapeDtypeStruct((2, keys // 2, D), jnp.bfloat16),
+            jax.ShapeDtypeStruct((keys // 2, D), jnp.bfloat16),
         ),
         in_specs=[
             pl.BlockSpec(memory_space=hbm),
@@ -421,7 +481,7 @@
             pl.BlockSpec(memory_space=hbm),
             pl.BlockSpec(memory_space=hbm),
         ],
-        out_specs=(pl.BlockSpec(memory_space=vmem),) * 3,
+        out_specs=(pl.BlockSpec(memory_space=vmem),) * 8,
         scratch_shapes=[
             smem(block_order.shape, jnp.int32),
             vmem((KV, rows, group * D), jnp.bfloat16),
@@ -452,11 +512,18 @@
     return pl.pallas_call(
         finish,
         out_shape=(jax.ShapeDtypeStruct(query.shape, jnp.bfloat16), stats),
-        in_specs=[pl.BlockSpec(memory_space=vmem)] * 3,
+        in_specs=[pl.BlockSpec(memory_space=vmem)] * 8,
         out_specs=(pl.BlockSpec(memory_space=hbm),) * 2,
-        scratch_shapes=[vmem((rows, heads), jnp.float32), dma((KV,)), dma],
-        compiler_params=pltpu.CompilerParams(vmem_limit_bytes=4 * 1024 * 1024),
-    )(out, total, top)
+        scratch_shapes=[
+            vmem((rows, group * D), jnp.bfloat16),
+            vmem((rows, heads), jnp.float32),
+            *work,
+            dma((KV - 1,)),
+            dma,
+            dma,
+        ],
+        compiler_params=pltpu.CompilerParams(vmem_limit_bytes=12 * 1024 * 1024),
+    )(*handed)
 
 
 def solution(mesh):

time: 32.2 us -> 31.6 us (0.981)
  Pallas kernels: 31.4 us -> 30.8 us
    pallas_call x1, Pallas kernels: 30 us -> 29.2 us  [body(): pl.pallas_call(functools.partial(kernel, n_ctx), out_shape=(jax.ShapeDtyp...]
where the time goes in v5:
time: 31.6 us; the launch traced here: 31.5 us
  Pallas kernels  30.8 us (97%)
  between operations  0.64 us (2%)
    pallas_call x1, Pallas kernels, body(): pl.pallas_call(functools.partial(kernel, n_ctx), out_shape=(jax.ShapeDtyp...  29.2 us
    pallas_call x1, Pallas kernels, body(): pl.pallas_call(finish, out_shape=(jax.ShapeDtypeStruct(query.shape, jnp.b...  1.65 us

profile of v5, /device:TPU:1, one launch (start us, length us, event | category | flops | bytes accessed | tf_op | source)
XLA Modules:
  0.0 31.5 jit_solution(325391921191662673)
XLA Ops:
  0.6 29.2 %shard_map.59 = (bf16[64,14336]{1,0:T(8,128)(2,1)S(1)}, f32[64,128]{1,0:T(8,128)S(1)}, f32[64,128]{1,0:T(8,128)S(1)}, bf16[64,2048]{1,0:T(8,128)(2,1)S(1)}, f32[...) custom-call(s32[256]{0:T(256)} %order_hbm.1, ...), custom_call_target="tpu_custom_call" | custom-call | flops 2147483648 | bytes 4194304 | tf_op jit(solution)/shard_map/pallas_call | solution.py:466
  29.8 1.6 %shard_map.60 = (bf16[64,16384]{1,0:T(8,128)(2,1)}, f32[64,128]{1,0:T(8,128)}) custom-call(bf16[64,14336]{1,0:T(8,128)(2,1)S(1)} %get-tuple-element.10.out_ref, f32[64,128]{1,0:T(8,128)S(1)} %get-tuple-element.11.total, f32[64,128]{1,0:T(8,128)S(1)} %get-tuple-element.12.top, bf16[64,2048]{1,0:T(8,128)(2,1)S(1)} %get-tuple-element.13.q, ...), custom_call_target="tpu_custom_call" | custom-call | tf_op jit(solution)/shard_map/pallas_call | solution.py:512

commit v6 on v5

--- a/solution.py
+++ b/solution.py
@@ -11,7 +11,7 @@
 D = 128
 KV = 8
 PLANE = 16
-AHEAD = 5
+AHEAD = 6
 RELAY = 3
 DIRECT = 4
 READY = 4
@@ -120,7 +120,7 @@
         return message(6, j, 2, 6, own_target)
 
     def to_relay(j):
-        stop = ctx - (PLANE - 1 - RELAY)
+        stop = (ctx + n_ctx - (PLANE - 1 - RELAY)) % n_ctx
         return pltpu.make_async_remote_copy(
             src_ref=chunk(0, j), dst_ref=relay_s.at[j],
             send_sem=send_sem.at[4, j], recv_sem=recv_sem.at[8, j],
@@ -365,15 +365,6 @@
 
     lax.fori_loop(0, KV - 1, far_step, 0)
 
-    end = KV - 1
-
-    @pl.when(direct(end))
-    def _():
-        arrived(6, end)
-
-    arrived(5, end)
-    arrived(7, end)
-    kv_last[...] = kv[end, :, keys:]
     def drain(j, carry):
         own_across(j).wait_send()
         own_partner(j).wait_send()
@@ -407,7 +398,18 @@
 
         return carry
 
-    lax.fori_loop(0, KV, drain, 0)
+    lax.fori_loop(0, KV - 1, drain, 0)
+
+    end = KV - 1
+
+    @pl.when(direct(end))
+    def _():
+        arrived(6, end)
+
+    arrived(5, end)
+    arrived(7, end)
+    kv_last[...] = kv[end, :, keys:]
+    drain(end, 0)
 
 
 def finish(out_ref, total, top, q, o, m, kv, mask, out_hbm, lse_hbm,

time: 31.6 us -> 31.6 us (level)
  no operation moved by 1% of the time
where the time goes in v6:
time: 31.6 us; the launch traced here: 31.5 us
  Pallas kernels  30.8 us (97%)
  between operations  0.64 us (2%)
    pallas_call x1, Pallas kernels, body(): pl.pallas_call(functools.partial(kernel, n_ctx), out_shape=(jax.ShapeDtyp...  29.2 us
    pallas_call x1, Pallas kernels, body(): pl.pallas_call(finish, out_shape=(jax.ShapeDtypeStruct(query.shape, jnp.b...  1.65 us

profile of v6, /device:TPU:1, one launch (start us, length us, event | category | flops | bytes accessed | tf_op | source)
XLA Modules:
  0.0 31.5 jit_solution(11262811382925945534)
XLA Ops:
  0.6 29.2 %shard_map.59 = (bf16[64,14336]{1,0:T(8,128)(2,1)S(1)}, f32[64,128]{1,0:T(8,128)S(1)}, f32[64,128]{1,0:T(8,128)S(1)}, bf16[64,2048]{1,0:T(8,128)(2,1)S(1)}, f32[...) custom-call(s32[256]{0:T(256)} %order_hbm.1, ...), custom_call_target="tpu_custom_call" | custom-call | flops 2147483648 | bytes 4194304 | tf_op jit(solution)/shard_map/pallas_call | solution.py:468
  29.8 1.7 %shard_map.60 = (bf16[64,16384]{1,0:T(8,128)(2,1)}, f32[64,128]{1,0:T(8,128)}) custom-call(bf16[64,14336]{1,0:T(8,128)(2,1)S(1)} %get-tuple-element.10.out_ref, f32[64,128]{1,0:T(8,128)S(1)} %get-tuple-element.11.total, f32[64,128]{1,0:T(8,128)S(1)} %get-tuple-element.12.top, bf16[64,2048]{1,0:T(8,128)(2,1)S(1)} %get-tuple-element.13.q, ...), custom_call_target="tpu_custom_call" | custom-call | tf_op jit(solution)/shard_map/pallas_call | solution.py:514
